TPU v7x, 512 devices: a whole 4x4x16 slice. The times are simulated.
512 devices in a mesh: grp: 4 (over x), gx: 8 (over y, core), gy: 16 (over z).
Axes of the slice: x: 4, y: 4, z: 16, core: 2. Of those that a mesh axis runs over, the one named last changes fastest.
Arguments:
- drive: float32 [3, 64, 1024, 128], P(None, ('grp', 'gx'), 'gy'), may hold values from -6 to 6
- permeability: float32 [48, 1024, 128], P('gx', 'gy'), may hold values from 0.5 to 8
Outputs:
- state: float32 [3, 64, 1024, 128], P(None, ('grp', 'gx'), 'gy')
All inputs are finite; a program needn't handle non-finite values.
Results may differ from a plain program's by a relative error of at most 0.0001.
Values sent between devices are 32-bit elements; how exact they have to be, the bound alone decides.
A program may use at most 64 MiB of HBM per device.

v0:
```python
import jax
import jax.numpy as jnp
from jax import lax
from jax.sharding import Mesh
from jax.sharding import PartitionSpec as P

SWEEPS = 4
OUTER = 2
GX = ("gx_0", "gx_1")
GRP_GX = ("grp", "gx_0", "gx_1")


relaxation = 0.8
pressure_rate = 0.5
interface_blend = 0.5


def extended(array, sides, width):
    edges = {}
    for axis, dim in sides:
        size, length = (lax.axis_size(axis), array.shape[dim])
        up = [(i, (i + 1) % size) for i in range(size - 1)]
        last = lax.slice_in_dim(array, length - width, length, axis=dim)
        leading = lax.slice_in_dim(array, 0, width, axis=dim)
        edges[dim] = (
            lax.ppermute(last, axis, up),
            lax.ppermute(leading, axis, [(b, a) for a, b in up]),
        )
    done = []
    for _, dim in sides:
        low, high = edges[dim]
        around = [(width, width) if d in done else (0, 0) for d in range(array.ndim)]
        array = jnp.concatenate([jnp.pad(low, around), array, jnp.pad(high, around)], axis=dim)
        done.append(dim)
    return array


def from_behind(block, axis, distance):
    devices = range(lax.axis_size(axis))
    route = [(i - distance, i) for i in devices if i - distance in devices]
    return lax.ppermute(block, axis, route)


def from_everyone(array, axis):
    length = lax.axis_size(axis)
    return lax.all_to_all(
        jnp.broadcast_to(array[None], (length, *array.shape)), axis, 0, 0, tiled=True
    )


def of_everyone(array, axis):
    everything = from_everyone(array, axis)
    return jnp.sum(everything, axis=0)


def over_axes(array, axes):
    far, near = axes
    nearer = of_everyone(array, near)
    return of_everyone(nearer, far)


def in_one(arrays, axis):
    ends = [0]
    for a in arrays:
        ends.append(ends[-1] + a.size)
    so_far = over_axes(jnp.concatenate([a.ravel() for a in arrays]), axis)
    return tuple((so_far[b:e].reshape(a.shape) for a, b, e in zip(arrays, ends, ends[1:])))


def shifted(fields, west_face, east_face, south_face, north_face, bottom):
    west_side = jnp.concatenate([west_face[:, None], fields[:, :-1]], axis=1)
    east_side = jnp.concatenate([fields[:, 1:], east_face[:, None]], axis=1)
    south_side = jnp.concatenate([south_face[:, :, None], fields[:, :, :-1]], axis=2)
    north_side = jnp.concatenate([fields[:, :, 1:], north_face[:, :, None]], axis=2)
    below_side = jnp.concatenate([bottom[:, :, :, None], fields[:, :, :, :-1]], axis=3)
    above_side = jnp.concatenate([fields[:, :, :, 1:], jnp.zeros_like(fields[:, :, :, :1])], axis=3)
    return (west_side, east_side, south_side, north_side, below_side, above_side)


def flow_sweep(flow_state, body_force, halo_set, inflow):
    zero_plane = jnp.zeros_like(inflow)
    bottom = jnp.stack([zero_plane, zero_plane, inflow, zero_plane])
    sides = shifted(flow_state, halo_set[0], halo_set[1], halo_set[2], halo_set[3], bottom)
    pressure = flow_state[3]
    gradient = jnp.stack([sides[1][3] - pressure, sides[3][3] - pressure, sides[5][3] - pressure])
    laplace = (
        sides[0][:3]
        + sides[1][:3]
        + sides[2][:3]
        + sides[3][:3]
        + sides[4][:3]
        + sides[5][:3]
        - 6.0 * flow_state[:3]
    )
    velocity = flow_state[:3] + relaxation / 6.0 * (body_force + laplace - gradient)
    divergence = (
        flow_state[0] - sides[0][0] + (flow_state[1] - sides[2][1]) + (flow_state[2] - sides[4][2])
    )
    pressure = pressure - pressure_rate * divergence
    return jnp.concatenate([velocity, pressure[None]], axis=0)


def bed_apply(field, weights, halo_set):
    bottom = jnp.zeros((1,) + field.shape[:2], jnp.float32)
    sides = shifted(
        field[None],
        halo_set[0][None],
        halo_set[1][None],
        halo_set[2][None],
        halo_set[3][None],
        bottom,
    )
    return weights[6] * field - (
        weights[0] * sides[0][0]
        + weights[1] * sides[1][0]
        + weights[2] * sides[2][0]
        + weights[3] * sides[3][0]
        + weights[4] * sides[4][0]
        + weights[5] * sides[5][0]
    )


def per_device(drive, permeability):
    group_index = lax.axis_index("grp")
    column = lax.axis_index(GX)
    row_index = lax.axis_index("gy")
    joined = lax.axis_index(GRP_GX)
    group_count = lax.axis_size("grp")
    columns_x = lax.axis_size(GX)
    columns_y = lax.axis_size("gy")
    is_bed = group_index == group_count - 1
    flow_count = (group_count - 1) * columns_x
    width_x = drive.shape[1]
    width_y = drive.shape[2]
    depth_z = drive.shape[3]
    bed_span = 3 * width_x
    source = drive.reshape(bed_span, width_y, depth_z)
    padded = extended(permeability, ((GX, 0), ("gy", 1)), 1)
    centre = padded[1:-1, 1:-1]
    extent = centre.shape
    x_place = lax.broadcasted_iota(jnp.int32, extent, 0)
    y_place = lax.broadcasted_iota(jnp.int32, extent, 1)
    z_place = lax.broadcasted_iota(jnp.int32, extent, 2)
    west_weight = jnp.where((x_place > 0) | (column > 0), (centre + padded[:-2, 1:-1]) * 0.5, 0.0)
    east_weight = jnp.where(
        (x_place < bed_span - 1) | (column < columns_x - 1), (centre + padded[2:, 1:-1]) * 0.5, 0.0
    )
    south_weight = jnp.where(
        (y_place > 0) | (row_index > 0), (centre + padded[1:-1, :-2]) * 0.5, 0.0
    )
    north_weight = jnp.where(
        (y_place < width_y - 1) | (row_index < columns_y - 1),
        (centre + padded[1:-1, 2:]) * 0.5,
        0.0,
    )
    zero_layer = jnp.zeros((extent[0], extent[1], 1), jnp.float32)
    below_perm = jnp.concatenate([zero_layer, centre[:, :, :-1]], axis=2)
    above_perm = jnp.concatenate([centre[:, :, 1:], zero_layer], axis=2)
    below_weight = jnp.where(z_place > 0, (centre + below_perm) * 0.5, 0.0)
    above_weight = jnp.where(z_place < depth_z - 1, (centre + above_perm) * 0.5, centre)
    centre_weight = (
        west_weight + east_weight + south_weight + north_weight + below_weight + above_weight
    )
    weights = (
        west_weight,
        east_weight,
        south_weight,
        north_weight,
        below_weight,
        above_weight,
        centre_weight,
    )
    west_open = jnp.where(is_bed, column > 0, True).astype(jnp.float32)
    east_open = jnp.where(is_bed, True, joined < flow_count - 1).astype(jnp.float32)

    def bed_halos(halo_set):
        return (
            halo_set[0][0],
            halo_set[1][0],
            halo_set[2][:3].reshape(bed_span, depth_z),
            halo_set[3][:3].reshape(bed_span, depth_z),
        )

    flow_state = jnp.zeros((4, width_x, width_y, depth_z), jnp.float32)
    inflow = jnp.zeros((width_x, width_y), jnp.float32)
    surface = jnp.zeros((bed_span, width_y), jnp.float32)
    solution = jnp.zeros_like(source)
    for outer_index in range(OUTER):
        rhs = source + jnp.where(z_place == depth_z - 1, centre * surface[:, :, None], 0.0)
        solution = jnp.zeros_like(source)
        resid = rhs
        direction = jnp.zeros_like(rhs)
        along = jnp.zeros_like(rhs)
        step_size = jnp.float32(1.0)
        norm_now = jnp.float32(1.0)
        for sweep_index in range(SWEEPS):
            grid = resid.reshape(3, width_x, width_y, depth_z)
            spare = jnp.zeros((1, width_x, depth_z), jnp.float32)
            west_out = jnp.where(is_bed, resid[0][None], flow_state[:, 0])
            south_out = jnp.where(
                is_bed, jnp.concatenate([grid[:, :, 0], spare], axis=0), flow_state[:, :, 0]
            )
            east_out = jnp.where(is_bed, resid[-1][None], flow_state[:3, -1])
            north_out = jnp.where(is_bed, grid[:, :, -1], flow_state[:3, :, -1])
            from_west = from_behind(east_out, GRP_GX, 1) * west_open
            from_east = from_behind(west_out, GRP_GX, -1) * east_open
            from_south = from_behind(north_out, "gy", 1)
            from_north = from_behind(south_out, "gy", -1)
            from_west = jnp.concatenate([from_west, jnp.zeros_like(from_west[:1])], axis=0)
            from_south = jnp.concatenate([from_south, jnp.zeros_like(from_south[:1])], axis=0)
            halo_set = (from_west, from_east, from_south, from_north)

            def bed_side(operands):
                bed_image = bed_apply(operands[1], weights, bed_halos(halo_set))
                return (
                    operands[0],
                    bed_image,
                    jnp.sum(operands[1] * operands[1]),
                    jnp.sum(operands[1] * bed_image),
                )

            def flow_side(operands):
                return (
                    flow_sweep(operands[0], drive, halo_set, inflow),
                    jnp.zeros_like(operands[1]),
                    jnp.float32(1.0),
                    jnp.float32(1.0),
                )

            flow_state, bed_image, first_part, second_part = lax.cond(
                is_bed, bed_side, flow_side, (flow_state, resid)
            )
            norm_next, product = in_one((first_part, second_part), ("gx_0", ("gx_1", "gy")))

            def advance(operands):
                moved, left_over, heading, image_sum, old_step = operands
                if sweep_index == 0:
                    new_step = norm_next / product
                    heading = left_over
                    image_sum = bed_image
                else:
                    ratio_now = norm_next / norm_now
                    new_step = norm_next / (product - ratio_now * norm_next / old_step)
                    heading = left_over + ratio_now * heading
                    image_sum = bed_image + ratio_now * image_sum
                return (
                    moved + new_step * heading,
                    left_over - new_step * image_sum,
                    heading,
                    image_sum,
                    new_step,
                )

            def keep_still(operands):
                return operands

            solution, resid, direction, along, step_size = lax.cond(
                is_bed, advance, keep_still, (solution, resid, direction, along, step_size)
            )
            norm_now = norm_next
        if outer_index + 1 < OUTER:
            pressure_plane = flow_state[3, :, :, 0]
            seep_plane = centre[:, :, -1] * solution[:, :, -1]
            bed_first = 3 * (joined - flow_count)
            slot_count = group_count * columns_x
            slot_place = lax.broadcasted_iota(jnp.int32, (slot_count, 1, 1), 0)
            flow_slot = flow_count + joined // 3
            bed_pieces = lax.dynamic_update_slice_in_dim(
                jnp.zeros((slot_count, width_x, width_y), jnp.float32),
                seep_plane.reshape(3, width_x, width_y),
                bed_first,
                0,
            )
            flow_pieces = jnp.where(slot_place == flow_slot, pressure_plane[None], 0.0)
            arrived = lax.all_to_all(
                jnp.where(is_bed, bed_pieces, flow_pieces),
                GRP_GX,
                split_axis=0,
                concat_axis=0,
                tiled=True,
            )
            arriving = lax.dynamic_index_in_dim(arrived, flow_slot, 0, keepdims=False)
            above_plane = lax.dynamic_slice_in_dim(arrived, bed_first, 3, 0).reshape(
                bed_span, width_y
            )
            inflow = arriving
            surface = interface_blend * above_plane + (1.0 - interface_blend) * surface
    return jnp.where(is_bed, solution.reshape(3, width_x, width_y, depth_z), flow_state[:3])


def solution(mesh):
    finer = Mesh(
        mesh.devices.reshape(mesh.shape["grp"], 4, 2, mesh.shape["gy"]),
        ("grp", "gx_0", "gx_1", "gy"),
    )
    return jax.shard_map(
        per_device,
        mesh=finer,
        in_specs=(P(None, GRP_GX, "gy", None), P(GX, "gy", None)),
        out_specs=P(None, GRP_GX, "gy", None),
        check_vma=False,
    )
```

profile of v0, /device:TPU:1, one launch (start us, length us, event | category | flops | bytes accessed | tf_op | source)
XLA Modules:
  0.0 410.3 jit_solution(6910358868315017898)
XLA Ops:
  0.8 4.6 %collective-permute-start.4 = (f32[1,64,128]{2,1,0:T(8,128)S(1)}, f32[1,64,128]{2,1,0:T(8,128)S(1)}, u32[]{:S(2)}, u32[]{:S(2)}) collective-permute-start(f32[1,64,128]{2,1,0:T(8,128)S(1)} %get-tuple-element.1317), channel_id=1, source_target_pairs={{0,16},{16,32},{32,48},{48,64},{64,80},{80,96},{96,112},{1,17},{17... | collective-permute-start | bytes 98312 | tf_op jit(solution)/shard_map/ppermute | solution.py:26
  5.4 5.5 %collective-permute-start.5 = (f32[1,64,128]{2,1,0:T(8,128)S(1)}, f32[1,64,128]{2,1,0:T(8,128)S(1)}, u32[]{:S(2)}, u32[]{:S(2)}) collective-permute-start(f32[1,64,128]{2,1,0:T(8,128)S(1)} %get-tuple-element.1318), channel_id=1, source_target_pairs={{16,0},{32,16},{48,32},{64,48},{80,64},{96,80},{112,96},{17,1},{33... | collective-permute-start | bytes 98312 | tf_op jit(solution)/shard_map/ppermute | solution.py:27
  24.6 4.2 %collective-permute-start.2 = (f32[3,2,128]{2,1,0:T(2,128)S(1)}, f32[3,2,128]{2,1,0:T(2,128)S(1)}, u32[]{:S(2)}, u32[]{:S(2)}) collective-permute-start(f32[3,2,128]{2,1,0:T(2,128)S(1)} %bitcast.816), channel_id=1, source_target_pairs={{0,1},{1,2},{2,3},{3,4},{4,5},{5,6},{6,7},{7,8},{8,9},{9,10},{10,1... | collective-permute-start | bytes 9224 | tf_op jit(solution)/shard_map/ppermute | solution.py:41
  30.4 18.9 %all-to-all-start = ((f32[32,1,2]{2,1,0:T(1,128)}), f32[32,1,2]{2,1,0:T(1,128)S(1)}, u32[]{:S(2)}, u32[]{:S(2)}) async-start(f32[32,1,2]{2,1,0:T(1,128)} %broadcast_in_dim.425), calls=%async_computation | async-start | bytes 32768 | tf_op jit(solution)/shard_map/all_to_all | solution.py:46
  49.5 11.7 %all-to-all-done = f32[32,1,2]{2,1,0:T(1,128)S(1)} async-done(((f32[32,1,2]{2,1,0:T(1,128)}), f32[32,1,2]{2,1,0:T(1,128)S(1)}, u32[]{:S(2)}, u32[]{:S(2)}) %all-to-all-start) | async-done | bytes 288 | tf_op jit(solution)/shard_map/all_to_all | solution.py:46
  61.3 8.7 %all_to_all.101 = f32[4,1,2]{2,1,0:T(1,128)S(1)} all-to-all(f32[4,1,2]{2,1,0:T(1,128)S(1)} %broadcast_in_dim.426), channel_id=1, replica_groups=mesh['grp'=4,'gx_0'=4,'gx_1'=2,'gy'=16] {'gx_0'}, dimensions={0} | all-to-all | bytes 64 | tf_op jit(solution)/shard_map/all_to_all | solution.py:46
  72.0 4.0 collective-permute-start.10
  76.0 4.5 %collective-permute-start.8 = (f32[3,64,128]{2,1,0:T(8,128)S(1)}, f32[3,64,128]{2,1,0:T(8,128)S(1)}, u32[]{:S(2)}, u32[]{:S(2)}) collective-permute-start(f32[3,64,128]{2,1,0:T(8,128)S(1)} %fusion.283), channel_id=1, source_target_pairs={{0,16},{16,32},{32,48},{48,64},{64,80},{80,96},{96,112},{112,128},... | collective-permute-start | bytes 294920 | tf_op jit(solution)/shard_map/ppermute | solution.py:41
  82.5 4.3 %collective-permute-done.9 = f32[4,64,128]{2,1,0:T(8,128)S(1)} collective-permute-done((f32[4,64,128]{2,1,0:T(8,128)S(1)}, f32[4,64,128]{2,1,0:T(8,128)S(1)}, u32[]{:S(2)}, u32[]{:S(2)}) %collective-permute-start.9) | collective-permute-done | bytes 131104 | tf_op jit(solution)/shard_map/ppermute | solution.py:41
  88.2 3.6 all-to-all-start.2
  92.0 11.7 %all-to-all-done.2 = f32[32,1,2]{2,1,0:T(1,128)S(1)} async-done(((f32[32,1,2]{2,1,0:T(1,128)}), f32[32,1,2]{2,1,0:T(1,128)S(1)}, u32[]{:S(2)}, u32[]{:S(2)}) %all-to-all-start.2) | async-done | bytes 288 | tf_op jit(solution)/shard_map/all_to_all | solution.py:46
  103.8 10.6 %all_to_all.102 = f32[4,1,2]{2,1,0:T(1,128)S(1)} all-to-all(f32[4,1,2]{2,1,0:T(1,128)S(1)} %broadcast_in_dim.432), channel_id=1, replica_groups=mesh['grp'=4,'gx_0'=4,'gx_1'=2,'gy'=16] {'gx_0'}, dimensions={0} | all-to-all | bytes 64 | tf_op jit(solution)/shard_map/all_to_all | solution.py:46
  115.8 4.0 collective-permute-start.14
  119.8 4.5 %collective-permute-start.12 = (f32[3,64,128]{2,1,0:T(8,128)S(1)}, f32[3,64,128]{2,1,0:T(8,128)S(1)}, u32[]{:S(2)}, u32[]{:S(2)}) collective-permute-start(f32[3,64,128]{2,1,0:T(8,128)S(1)} %fusion.282), channel_id=1, source_target_pairs={{0,16},{16,32},{32,48},{48,64},{64,80},{80,96},{96,112},{112,128},... | collective-permute-start | bytes 294920 | tf_op jit(solution)/shard_map/ppermute | solution.py:41
  126.3 4.3 %collective-permute-done.13 = f32[4,64,128]{2,1,0:T(8,128)S(1)} collective-permute-done((f32[4,64,128]{2,1,0:T(8,128)S(1)}, f32[4,64,128]{2,1,0:T(8,128)S(1)}, u32[]{:S(2)}, u32[]{:S(2)}) %collective-permute-start.13) | collective-permute-done | bytes 131104 | tf_op jit(solution)/shard_map/ppermute | solution.py:41
  131.9 3.6 all-to-all-start.4
  135.8 11.7 %all-to-all-done.4 = f32[32,1,2]{2,1,0:T(1,128)S(1)} async-done(((f32[32,1,2]{2,1,0:T(1,128)}), f32[32,1,2]{2,1,0:T(1,128)S(1)}, u32[]{:S(2)}, u32[]{:S(2)}) %all-to-all-start.4) | async-done | bytes 288 | tf_op jit(solution)/shard_map/all_to_all | solution.py:46
  147.5 10.6 %all_to_all.103 = f32[4,1,2]{2,1,0:T(1,128)S(1)} all-to-all(f32[4,1,2]{2,1,0:T(1,128)S(1)} %broadcast_in_dim.438), channel_id=1, replica_groups=mesh['grp'=4,'gx_0'=4,'gx_1'=2,'gy'=16] {'gx_0'}, dimensions={0} | all-to-all | bytes 64 | tf_op jit(solution)/shard_map/all_to_all | solution.py:46
  159.6 4.0 collective-permute-start.18
  163.6 4.5 %collective-permute-start.16 = (f32[3,64,128]{2,1,0:T(8,128)S(1)}, f32[3,64,128]{2,1,0:T(8,128)S(1)}, u32[]{:S(2)}, u32[]{:S(2)}) collective-permute-start(f32[3,64,128]{2,1,0:T(8,128)S(1)} %fusion.281), channel_id=1, source_target_pairs={{0,16},{16,32},{32,48},{48,64},{64,80},{80,96},{96,112},{112,128},... | collective-permute-start | bytes 294920 | tf_op jit(solution)/shard_map/ppermute | solution.py:41
  170.0 4.3 %collective-permute-done.17 = f32[4,64,128]{2,1,0:T(8,128)S(1)} collective-permute-done((f32[4,64,128]{2,1,0:T(8,128)S(1)}, f32[4,64,128]{2,1,0:T(8,128)S(1)}, u32[]{:S(2)}, u32[]{:S(2)}) %collective-permute-start.17) | collective-permute-done | bytes 131104 | tf_op jit(solution)/shard_map/ppermute | solution.py:41
  179.4 11.8 %all-to-all-done.6 = f32[32,1,2]{2,1,0:T(1,128)S(1)} async-done(((f32[32,1,2]{2,1,0:T(1,128)}), f32[32,1,2]{2,1,0:T(1,128)S(1)}, u32[]{:S(2)}, u32[]{:S(2)}) %all-to-all-start.6) | async-done | bytes 288 | tf_op jit(solution)/shard_map/all_to_all | solution.py:46
  191.3 14.0 %all_to_all.104 = f32[4,1,2]{2,1,0:T(1,128)S(1)} all-to-all(f32[4,1,2]{2,1,0:T(1,128)S(1)} %broadcast_in_dim.444), channel_id=1, replica_groups=mesh['grp'=4,'gx_0'=4,'gx_1'=2,'gy'=16] {'gx_0'}, dimensions={0} | all-to-all | bytes 64 | tf_op jit(solution)/shard_map/all_to_all | solution.py:46
  206.5 11.9 %all-to-all-start.8 = ((f32[32,1,128]{2,1,0:T(1,128)}), f32[32,1,128]{2,1,0:T(1,128)S(1)}, u32[]{:S(2)}, u32[]{:S(2)}) async-start(f32[32,1,128]{2,1,0:T(1,128)} %reshape.376), calls=%async_computation.8 | async-start | bytes 32768 | tf_op jit(solution)/shard_map/all_to_all | solution.py:275
  218.6 6.7 %all-to-all-done.8 = f32[32,1,128]{2,1,0:T(1,128)S(1)} async-done(((f32[32,1,128]{2,1,0:T(1,128)}), f32[32,1,128]{2,1,0:T(1,128)S(1)}, u32[]{:S(2)}, u32[]{:S(2)}) %all-to-all-start.8) | async-done | bytes 16416 | tf_op jit(solution)/shard_map/all_to_all | solution.py:275
  228.1 4.0 collective-permute-start.22
  244.2 3.6 all-to-all-start.9
  248.1 11.7 %all-to-all-done.9 = f32[32,1,2]{2,1,0:T(1,128)S(1)} async-done(((f32[32,1,2]{2,1,0:T(1,128)}), f32[32,1,2]{2,1,0:T(1,128)S(1)}, u32[]{:S(2)}, u32[]{:S(2)}) %all-to-all-start.9) | async-done | bytes 288 | tf_op jit(solution)/shard_map/all_to_all | solution.py:46
  259.9 8.2 %all_to_all.105 = f32[4,1,2]{2,1,0:T(1,128)S(1)} all-to-all(f32[4,1,2]{2,1,0:T(1,128)S(1)} %broadcast_in_dim.453), channel_id=1, replica_groups=mesh['grp'=4,'gx_0'=4,'gx_1'=2,'gy'=16] {'gx_0'}, dimensions={0} | all-to-all | bytes 64 | tf_op jit(solution)/shard_map/all_to_all | solution.py:46
  270.1 4.0 collective-permute-start.26
  274.1 4.5 %collective-permute-start.24 = (f32[3,64,128]{2,1,0:T(8,128)S(1)}, f32[3,64,128]{2,1,0:T(8,128)S(1)}, u32[]{:S(2)}, u32[]{:S(2)}) collective-permute-start(f32[3,64,128]{2,1,0:T(8,128)S(1)} %fusion.279), channel_id=1, source_target_pairs={{0,16},{16,32},{32,48},{48,64},{64,80},{80,96},{96,112},{112,128},... | collective-permute-start | bytes 294920 | tf_op jit(solution)/shard_map/ppermute | solution.py:41
  281.2 3.7 collective-permute-done.25
  285.6 4.4 %conditional.26 = (f32[4,2,64,128]{3,2,1,0:T(8,128)S(1)}, f32[6,64,128]{2,1,0:T(8,128)S(1)}, f32[]{:T(128)}, f32[]{:T(128)}) conditional(s32[]{:T(128)} %convert_element_type.9, (f32[4,2,64,128]{3,2,1,0:T(8,128)S(1)}, f32[3,64,128]{2,1,0:T(8,128)}, f32[4,64,128]{2,1,0:T(8,128)}, f32[3,2,128]{2,1,0:T(2,128)S(1)}, f32[4,2,128]{2,1,0:T(2,128)S(1)}, ...), branch_computations={%region_40.41_spmd, %region_41.44_spmd} | conditional | flops 1197056 | bytes 11667236 | solution.py:230
  290.7 3.6 all-to-all-start.11
  294.5 11.7 %all-to-all-done.11 = f32[32,1,2]{2,1,0:T(1,128)S(1)} async-done(((f32[32,1,2]{2,1,0:T(1,128)}), f32[32,1,2]{2,1,0:T(1,128)S(1)}, u32[]{:S(2)}, u32[]{:S(2)}) %all-to-all-start.11) | async-done | bytes 288 | tf_op jit(solution)/shard_map/all_to_all | solution.py:46
  306.3 12.5 %all_to_all.106 = f32[4,1,2]{2,1,0:T(1,128)S(1)} all-to-all(f32[4,1,2]{2,1,0:T(1,128)S(1)} %broadcast_in_dim.459), channel_id=1, replica_groups=mesh['grp'=4,'gx_0'=4,'gx_1'=2,'gy'=16] {'gx_0'}, dimensions={0} | all-to-all | bytes 64 | tf_op jit(solution)/shard_map/all_to_all | solution.py:46
  320.2 4.0 collective-permute-start.30
  324.2 4.5 %collective-permute-start.28 = (f32[3,64,128]{2,1,0:T(8,128)S(1)}, f32[3,64,128]{2,1,0:T(8,128)S(1)}, u32[]{:S(2)}, u32[]{:S(2)}) collective-permute-start(f32[3,64,128]{2,1,0:T(8,128)S(1)} %fusion.278), channel_id=1, source_target_pairs={{0,16},{16,32},{32,48},{48,64},{64,80},{80,96},{96,112},{112,128},... | collective-permute-start | bytes 294920 | tf_op jit(solution)/shard_map/ppermute | solution.py:41
  331.3 3.7 collective-permute-done.29
  335.7 4.4 %conditional.28 = (f32[4,2,64,128]{3,2,1,0:T(8,128)S(1)}, f32[6,64,128]{2,1,0:T(8,128)S(1)}, f32[]{:T(128)}, f32[]{:T(128)}) conditional(s32[]{:T(128)} %convert_element_type.9, (f32[4,2,64,128]{3,2,1,0:T(8,128)S(1)}, f32[3,64,128]{2,1,0:T(8,128)}, f32[4,64,128]{2,1,0:T(8,128)}, f32[3,2,128]{2,1,0:T(2,128)S(1)}, f32[4,2,128]{2,1,0:T(2,128)S(1)}, ...), branch_computations={%region_48.49_spmd, %region_49.52_spmd} | conditional | flops 1197056 | bytes 11667236 | solution.py:230
  340.7 3.7 all-to-all-start.13
  344.6 11.7 %all-to-all-done.13 = f32[32,1,2]{2,1,0:T(1,128)S(1)} async-done(((f32[32,1,2]{2,1,0:T(1,128)}), f32[32,1,2]{2,1,0:T(1,128)S(1)}, u32[]{:S(2)}, u32[]{:S(2)}) %all-to-all-start.13) | async-done | bytes 288 | tf_op jit(solution)/shard_map/all_to_all | solution.py:46
  356.4 9.8 %all_to_all.107 = f32[4,1,2]{2,1,0:T(1,128)S(1)} all-to-all(f32[4,1,2]{2,1,0:T(1,128)S(1)} %broadcast_in_dim.465), channel_id=1, replica_groups=mesh['grp'=4,'gx_0'=4,'gx_1'=2,'gy'=16] {'gx_0'}, dimensions={0} | all-to-all | bytes 64 | tf_op jit(solution)/shard_map/all_to_all | solution.py:46
  367.5 4.0 collective-permute-start.34
  371.5 4.5 %collective-permute-start.32 = (f32[3,64,128]{2,1,0:T(8,128)S(1)}, f32[3,64,128]{2,1,0:T(8,128)S(1)}, u32[]{:S(2)}, u32[]{:S(2)}) collective-permute-start(f32[3,64,128]{2,1,0:T(8,128)S(1)} %fusion.277), channel_id=1, source_target_pairs={{0,16},{16,32},{32,48},{48,64},{64,80},{80,96},{96,112},{112,128},... | collective-permute-start | bytes 294920 | tf_op jit(solution)/shard_map/ppermute | solution.py:41
  378.0 4.3 %collective-permute-done.33 = f32[4,64,128]{2,1,0:T(8,128)S(1)} collective-permute-done((f32[4,64,128]{2,1,0:T(8,128)S(1)}, f32[4,64,128]{2,1,0:T(8,128)S(1)}, u32[]{:S(2)}, u32[]{:S(2)}) %collective-permute-start.33) | collective-permute-done | bytes 131104 | tf_op jit(solution)/shard_map/ppermute | solution.py:41
  383.3 15.4 %all_to_all.108 = f32[32,1,2]{2,1,0:T(1,128)S(1)} all-to-all(f32[32,1,2]{2,1,0:T(1,128)S(1)} %broadcast_in_dim.470), channel_id=1, replica_groups=mesh['grp'=4,'gx_0'=4,'gx_1'=2,'gy'=16] {'gx_1','gy'}, dimensions={0} | all-to-all | bytes 512 | tf_op jit(solution)/shard_map/all_to_all | solution.py:46
  398.8 10.8 %all_to_all.109 = f32[4,1,2]{2,1,0:T(1,128)S(1)} all-to-all(f32[4,1,2]{2,1,0:T(1,128)S(1)} %broadcast_in_dim.471), channel_id=1, replica_groups=mesh['grp'=4,'gx_0'=4,'gx_1'=2,'gy'=16] {'gx_0'}, dimensions={0} | all-to-all | bytes 64 | tf_op jit(solution)/shard_map/all_to_all | solution.py:46
  (317 shorter events, 82.3 us)
Async XLA Ops:
  0.8 14.7 %collective-permute-start.4 = (f32[1,64,128]{2,1,0:T(8,128)S(1)}, f32[1,64,128]{2,1,0:T(8,128)S(1)}, u32[]{:S(2)}, u32[]{:S(2)}) collective-permute-start(f32[1,64,128]{2,1,0:T(8,128)S(1)} %get-tuple-element.1317), channel_id=1, source_target_pairs={{0,16},{16,32},{32,48},{48,64},{64,80},{80,96},{96,112},{1,17},{17... | collective-permute-start | bytes 98312 | tf_op jit(solution)/shard_map/ppermute | solution.py:26
  5.4 10.2 %collective-permute-start.5 = (f32[1,64,128]{2,1,0:T(8,128)S(1)}, f32[1,64,128]{2,1,0:T(8,128)S(1)}, u32[]{:S(2)}, u32[]{:S(2)}) collective-permute-start(f32[1,64,128]{2,1,0:T(8,128)S(1)} %get-tuple-element.1318), channel_id=1, source_target_pairs={{16,0},{32,16},{48,32},{64,48},{80,64},{96,80},{112,96},{17,1},{33... | collective-permute-start | bytes 98312 | tf_op jit(solution)/shard_map/ppermute | solution.py:27
  11.6 4.0 collective-permute-start.6
  12.9 4.5 %collective-permute-start.7 = (f32[6,1,128]{2,1,0:T(1,128)S(1)}, f32[6,1,128]{2,1,0:T(1,128)S(1)}, u32[]{:S(2)}, u32[]{:S(2)}) collective-permute-start(f32[6,1,128]{2,1,0:T(1,128)S(1)} %get-tuple-element.1315), channel_id=1, source_target_pairs={{1,0},{2,1},{3,2},{4,3},{5,4},{6,5},{7,6},{8,7},{9,8},{10,9},{11,1... | collective-permute-start | bytes 9224 | tf_op jit(solution)/shard_map/ppermute | solution.py:27
  14.2 1.3 copy-start.1
  15.5 1.9 copy-start
  17.7 11.1 %collective-permute-start.1 = (f32[4,64,128]{2,1,0:T(8,128)S(1)}, f32[4,64,128]{2,1,0:T(8,128)S(1)}, u32[]{:S(2)}, u32[]{:S(2)}) collective-permute-start(f32[4,64,128]{2,1,0:T(8,128)S(1)} %broadcast_in_dim.424), channel_id=1, source_target_pairs={{16,0},{32,16},{48,32},{64,48},{80,64},{96,80},{112,96},{128,112},... | collective-permute-start | bytes 393224 | tf_op jit(solution)/shard_map/ppermute | solution.py:41
  20.0 8.8 %collective-permute-start = (f32[3,64,128]{2,1,0:T(8,128)S(1)}, f32[3,64,128]{2,1,0:T(8,128)S(1)}, u32[]{:S(2)}, u32[]{:S(2)}) collective-permute-start(f32[3,64,128]{2,1,0:T(8,128)S(1)} %broadcast_in_dim.423), channel_id=1, source_target_pairs={{0,16},{16,32},{32,48},{48,64},{64,80},{80,96},{96,112},{112,128},... | collective-permute-start | bytes 294920 | tf_op jit(solution)/shard_map/ppermute | solution.py:41
  23.3 6.2 %collective-permute-start.3 = (f32[4,2,128]{2,1,0:T(2,128)S(1)}, f32[4,2,128]{2,1,0:T(2,128)S(1)}, u32[]{:S(2)}, u32[]{:S(2)}) collective-permute-start(f32[4,2,128]{2,1,0:T(2,128)S(1)} %pad_select_fusion.2), channel_id=1, source_target_pairs={{1,0},{2,1},{3,2},{4,3},{5,4},{6,5},{7,6},{8,7},{9,8},{10,9},{11,1... | collective-permute-start | bytes 12296 | tf_op jit(solution)/shard_map/ppermute | solution.py:41
  24.6 4.9 %collective-permute-start.2 = (f32[3,2,128]{2,1,0:T(2,128)S(1)}, f32[3,2,128]{2,1,0:T(2,128)S(1)}, u32[]{:S(2)}, u32[]{:S(2)}) collective-permute-start(f32[3,2,128]{2,1,0:T(2,128)S(1)} %bitcast.816), channel_id=1, source_target_pairs={{0,1},{1,2},{2,3},{3,4},{4,5},{5,6},{6,7},{7,8},{8,9},{9,10},{10,1... | collective-permute-start | bytes 9224 | tf_op jit(solution)/shard_map/ppermute | solution.py:41
  30.4 30.8 %all-to-all-start = ((f32[32,1,2]{2,1,0:T(1,128)}), f32[32,1,2]{2,1,0:T(1,128)S(1)}, u32[]{:S(2)}, u32[]{:S(2)}) async-start(f32[32,1,2]{2,1,0:T(1,128)} %broadcast_in_dim.425), calls=%async_computation | async-start | bytes 32768 | tf_op jit(solution)/shard_map/all_to_all | solution.py:46
  70.7 16.1 %collective-permute-start.11 = (f32[4,2,128]{2,1,0:T(2,128)S(1)}, f32[4,2,128]{2,1,0:T(2,128)S(1)}, u32[]{:S(2)}, u32[]{:S(2)}) collective-permute-start(f32[4,2,128]{2,1,0:T(2,128)S(1)} %fusion.292), channel_id=1, source_target_pairs={{1,0},{2,1},{3,2},{4,3},{5,4},{6,5},{7,6},{8,7},{9,8},{10,9},{11,1... | collective-permute-start | bytes 12296 | tf_op jit(solution)/shard_map/ppermute | solution.py:41
  72.0 14.8 %collective-permute-start.10 = (f32[3,2,128]{2,1,0:T(2,128)S(1)}, f32[3,2,128]{2,1,0:T(2,128)S(1)}, u32[]{:S(2)}, u32[]{:S(2)}) collective-permute-start(f32[3,2,128]{2,1,0:T(2,128)S(1)} %bitcast.819), channel_id=1, source_target_pairs={{0,1},{1,2},{2,3},{3,4},{4,5},{5,6},{6,7},{7,8},{8,9},{9,10},{10,1... | collective-permute-start | bytes 9224 | tf_op jit(solution)/shard_map/ppermute | solution.py:41
  76.0 6.4 %collective-permute-start.8 = (f32[3,64,128]{2,1,0:T(8,128)S(1)}, f32[3,64,128]{2,1,0:T(8,128)S(1)}, u32[]{:S(2)}, u32[]{:S(2)}) collective-permute-start(f32[3,64,128]{2,1,0:T(8,128)S(1)} %fusion.283), channel_id=1, source_target_pairs={{0,16},{16,32},{32,48},{48,64},{64,80},{80,96},{96,112},{112,128},... | collective-permute-start | bytes 294920 | tf_op jit(solution)/shard_map/ppermute | solution.py:41
  80.6 6.3 %collective-permute-start.9 = (f32[4,64,128]{2,1,0:T(8,128)S(1)}, f32[4,64,128]{2,1,0:T(8,128)S(1)}, u32[]{:S(2)}, u32[]{:S(2)}) collective-permute-start(f32[4,64,128]{2,1,0:T(8,128)S(1)} %fusion.276), channel_id=1, source_target_pairs={{16,0},{32,16},{48,32},{64,48},{80,64},{96,80},{112,96},{128,112},... | collective-permute-start | bytes 393224 | tf_op jit(solution)/shard_map/ppermute | solution.py:41
  88.2 15.6 %all-to-all-start.2 = ((f32[32,1,2]{2,1,0:T(1,128)}), f32[32,1,2]{2,1,0:T(1,128)S(1)}, u32[]{:S(2)}, u32[]{:S(2)}) async-start(f32[32,1,2]{2,1,0:T(1,128)} %broadcast_in_dim.431), calls=%async_computation.2 | async-start | bytes 32768 | tf_op jit(solution)/shard_map/all_to_all | solution.py:46
  114.5 16.1 %collective-permute-start.15 = (f32[4,2,128]{2,1,0:T(2,128)S(1)}, f32[4,2,128]{2,1,0:T(2,128)S(1)}, u32[]{:S(2)}, u32[]{:S(2)}) collective-permute-start(f32[4,2,128]{2,1,0:T(2,128)S(1)} %fusion.291), channel_id=1, source_target_pairs={{1,0},{2,1},{3,2},{4,3},{5,4},{6,5},{7,6},{8,7},{9,8},{10,9},{11,1... | collective-permute-start | bytes 12296 | tf_op jit(solution)/shard_map/ppermute | solution.py:41
  115.8 14.8 %collective-permute-start.14 = (f32[3,2,128]{2,1,0:T(2,128)S(1)}, f32[3,2,128]{2,1,0:T(2,128)S(1)}, u32[]{:S(2)}, u32[]{:S(2)}) collective-permute-start(f32[3,2,128]{2,1,0:T(2,128)S(1)} %bitcast.820), channel_id=1, source_target_pairs={{0,1},{1,2},{2,3},{3,4},{4,5},{5,6},{6,7},{7,8},{8,9},{9,10},{10,1... | collective-permute-start | bytes 9224 | tf_op jit(solution)/shard_map/ppermute | solution.py:41
  119.8 6.4 %collective-permute-start.12 = (f32[3,64,128]{2,1,0:T(8,128)S(1)}, f32[3,64,128]{2,1,0:T(8,128)S(1)}, u32[]{:S(2)}, u32[]{:S(2)}) collective-permute-start(f32[3,64,128]{2,1,0:T(8,128)S(1)} %fusion.282), channel_id=1, source_target_pairs={{0,16},{16,32},{32,48},{48,64},{64,80},{80,96},{96,112},{112,128},... | collective-permute-start | bytes 294920 | tf_op jit(solution)/shard_map/ppermute | solution.py:41
  124.3 6.3 %collective-permute-start.13 = (f32[4,64,128]{2,1,0:T(8,128)S(1)}, f32[4,64,128]{2,1,0:T(8,128)S(1)}, u32[]{:S(2)}, u32[]{:S(2)}) collective-permute-start(f32[4,64,128]{2,1,0:T(8,128)S(1)} %fusion.275), channel_id=1, source_target_pairs={{16,0},{32,16},{48,32},{64,48},{80,64},{96,80},{112,96},{128,112},... | collective-permute-start | bytes 393224 | tf_op jit(solution)/shard_map/ppermute | solution.py:41
  131.9 15.6 %all-to-all-start.4 = ((f32[32,1,2]{2,1,0:T(1,128)}), f32[32,1,2]{2,1,0:T(1,128)S(1)}, u32[]{:S(2)}, u32[]{:S(2)}) async-start(f32[32,1,2]{2,1,0:T(1,128)} %broadcast_in_dim.437), calls=%async_computation.4 | async-start | bytes 32768 | tf_op jit(solution)/shard_map/all_to_all | solution.py:46
  158.3 16.1 %collective-permute-start.19 = (f32[4,2,128]{2,1,0:T(2,128)S(1)}, f32[4,2,128]{2,1,0:T(2,128)S(1)}, u32[]{:S(2)}, u32[]{:S(2)}) collective-permute-start(f32[4,2,128]{2,1,0:T(2,128)S(1)} %fusion.290), channel_id=1, source_target_pairs={{1,0},{2,1},{3,2},{4,3},{5,4},{6,5},{7,6},{8,7},{9,8},{10,9},{11,1... | collective-permute-start | bytes 12296 | tf_op jit(solution)/shard_map/ppermute | solution.py:41
  159.6 14.8 %collective-permute-start.18 = (f32[3,2,128]{2,1,0:T(2,128)S(1)}, f32[3,2,128]{2,1,0:T(2,128)S(1)}, u32[]{:S(2)}, u32[]{:S(2)}) collective-permute-start(f32[3,2,128]{2,1,0:T(2,128)S(1)} %bitcast.821), channel_id=1, source_target_pairs={{0,1},{1,2},{2,3},{3,4},{4,5},{5,6},{6,7},{7,8},{8,9},{9,10},{10,1... | collective-permute-start | bytes 9224 | tf_op jit(solution)/shard_map/ppermute | solution.py:41
  163.6 6.4 %collective-permute-start.16 = (f32[3,64,128]{2,1,0:T(8,128)S(1)}, f32[3,64,128]{2,1,0:T(8,128)S(1)}, u32[]{:S(2)}, u32[]{:S(2)}) collective-permute-start(f32[3,64,128]{2,1,0:T(8,128)S(1)} %fusion.281), channel_id=1, source_target_pairs={{0,16},{16,32},{32,48},{48,64},{64,80},{80,96},{96,112},{112,128},... | collective-permute-start | bytes 294920 | tf_op jit(solution)/shard_map/ppermute | solution.py:41
  168.1 6.3 %collective-permute-start.17 = (f32[4,64,128]{2,1,0:T(8,128)S(1)}, f32[4,64,128]{2,1,0:T(8,128)S(1)}, u32[]{:S(2)}, u32[]{:S(2)}) collective-permute-start(f32[4,64,128]{2,1,0:T(8,128)S(1)} %fusion.274), channel_id=1, source_target_pairs={{16,0},{32,16},{48,32},{64,48},{80,64},{96,80},{112,96},{128,112},... | collective-permute-start | bytes 393224 | tf_op jit(solution)/shard_map/ppermute | solution.py:41
  175.7 15.6 %all-to-all-start.6 = ((f32[32,1,2]{2,1,0:T(1,128)}), f32[32,1,2]{2,1,0:T(1,128)S(1)}, u32[]{:S(2)}, u32[]{:S(2)}) async-start(f32[32,1,2]{2,1,0:T(1,128)} %broadcast_in_dim.443), calls=%async_computation.6 | async-start | bytes 32768 | tf_op jit(solution)/shard_map/all_to_all | solution.py:46
  206.5 18.8 %all-to-all-start.8 = ((f32[32,1,128]{2,1,0:T(1,128)}), f32[32,1,128]{2,1,0:T(1,128)S(1)}, u32[]{:S(2)}, u32[]{:S(2)}) async-start(f32[32,1,128]{2,1,0:T(1,128)} %reshape.376), calls=%async_computation.8 | async-start | bytes 32768 | tf_op jit(solution)/shard_map/all_to_all | solution.py:275
  226.8 13.2 %collective-permute-start.23 = (f32[4,2,128]{2,1,0:T(2,128)S(1)}, f32[4,2,128]{2,1,0:T(2,128)S(1)}, u32[]{:S(2)}, u32[]{:S(2)}) collective-permute-start(f32[4,2,128]{2,1,0:T(2,128)S(1)} %fusion.289), channel_id=1, source_target_pairs={{1,0},{2,1},{3,2},{4,3},{5,4},{6,5},{7,6},{8,7},{9,8},{10,9},{11,1... | collective-permute-start | bytes 12296 | tf_op jit(solution)/shard_map/ppermute | solution.py:41
  228.1 11.9 %collective-permute-start.22 = (f32[3,2,128]{2,1,0:T(2,128)S(1)}, f32[3,2,128]{2,1,0:T(2,128)S(1)}, u32[]{:S(2)}, u32[]{:S(2)}) collective-permute-start(f32[3,2,128]{2,1,0:T(2,128)S(1)} %bitcast.817), channel_id=1, source_target_pairs={{0,1},{1,2},{2,3},{3,4},{4,5},{5,6},{6,7},{7,8},{8,9},{9,10},{10,1... | collective-permute-start | bytes 9224 | tf_op jit(solution)/shard_map/ppermute | solution.py:41
  232.1 7.9 %collective-permute-start.21 = (f32[4,64,128]{2,1,0:T(8,128)S(1)}, f32[4,64,128]{2,1,0:T(8,128)S(1)}, u32[]{:S(2)}, u32[]{:S(2)}) collective-permute-start(f32[4,64,128]{2,1,0:T(8,128)S(1)} %fusion.273), channel_id=1, source_target_pairs={{16,0},{32,16},{48,32},{64,48},{80,64},{96,80},{112,96},{128,112},... | collective-permute-start | bytes 393224 | tf_op jit(solution)/shard_map/ppermute | solution.py:41
  235.2 4.1 collective-permute-start.20
  244.2 15.6 %all-to-all-start.9 = ((f32[32,1,2]{2,1,0:T(1,128)}), f32[32,1,2]{2,1,0:T(1,128)S(1)}, u32[]{:S(2)}, u32[]{:S(2)}) async-start(f32[32,1,2]{2,1,0:T(1,128)} %broadcast_in_dim.452), calls=%async_computation.9 | async-start | bytes 32768 | tf_op jit(solution)/shard_map/all_to_all | solution.py:46
  268.8 16.8 %collective-permute-start.27 = (f32[4,2,128]{2,1,0:T(2,128)S(1)}, f32[4,2,128]{2,1,0:T(2,128)S(1)}, u32[]{:S(2)}, u32[]{:S(2)}) collective-permute-start(f32[4,2,128]{2,1,0:T(2,128)S(1)} %fusion.288), channel_id=1, source_target_pairs={{1,0},{2,1},{3,2},{4,3},{5,4},{6,5},{7,6},{8,7},{9,8},{10,9},{11,1... | collective-permute-start | bytes 12296 | tf_op jit(solution)/shard_map/ppermute | solution.py:41
  270.1 15.5 %collective-permute-start.26 = (f32[3,2,128]{2,1,0:T(2,128)S(1)}, f32[3,2,128]{2,1,0:T(2,128)S(1)}, u32[]{:S(2)}, u32[]{:S(2)}) collective-permute-start(f32[3,2,128]{2,1,0:T(2,128)S(1)} %bitcast.822), channel_id=1, source_target_pairs={{0,1},{1,2},{2,3},{3,4},{4,5},{5,6},{6,7},{7,8},{8,9},{9,10},{10,1... | collective-permute-start | bytes 9224 | tf_op jit(solution)/shard_map/ppermute | solution.py:41
  274.1 6.4 %collective-permute-start.24 = (f32[3,64,128]{2,1,0:T(8,128)S(1)}, f32[3,64,128]{2,1,0:T(8,128)S(1)}, u32[]{:S(2)}, u32[]{:S(2)}) collective-permute-start(f32[3,64,128]{2,1,0:T(8,128)S(1)} %fusion.279), channel_id=1, source_target_pairs={{0,16},{16,32},{32,48},{48,64},{64,80},{80,96},{96,112},{112,128},... | collective-permute-start | bytes 294920 | tf_op jit(solution)/shard_map/ppermute | solution.py:41
  278.6 6.3 %collective-permute-start.25 = (f32[4,64,128]{2,1,0:T(8,128)S(1)}, f32[4,64,128]{2,1,0:T(8,128)S(1)}, u32[]{:S(2)}, u32[]{:S(2)}) collective-permute-start(f32[4,64,128]{2,1,0:T(8,128)S(1)} %fusion.272), channel_id=1, source_target_pairs={{16,0},{32,16},{48,32},{64,48},{80,64},{96,80},{112,96},{128,112},... | collective-permute-start | bytes 393224 | tf_op jit(solution)/shard_map/ppermute | solution.py:41
  288.6 1.2 copy-start.11
  290.7 15.6 %all-to-all-start.11 = ((f32[32,1,2]{2,1,0:T(1,128)}), f32[32,1,2]{2,1,0:T(1,128)S(1)}, u32[]{:S(2)}, u32[]{:S(2)}) async-start(f32[32,1,2]{2,1,0:T(1,128)} %broadcast_in_dim.458), calls=%async_computation.11 | async-start | bytes 32768 | tf_op jit(solution)/shard_map/all_to_all | solution.py:46
  318.9 16.8 %collective-permute-start.31 = (f32[4,2,128]{2,1,0:T(2,128)S(1)}, f32[4,2,128]{2,1,0:T(2,128)S(1)}, u32[]{:S(2)}, u32[]{:S(2)}) collective-permute-start(f32[4,2,128]{2,1,0:T(2,128)S(1)} %fusion.287), channel_id=1, source_target_pairs={{1,0},{2,1},{3,2},{4,3},{5,4},{6,5},{7,6},{8,7},{9,8},{10,9},{11,1... | collective-permute-start | bytes 12296 | tf_op jit(solution)/shard_map/ppermute | solution.py:41
  320.2 15.5 %collective-permute-start.30 = (f32[3,2,128]{2,1,0:T(2,128)S(1)}, f32[3,2,128]{2,1,0:T(2,128)S(1)}, u32[]{:S(2)}, u32[]{:S(2)}) collective-permute-start(f32[3,2,128]{2,1,0:T(2,128)S(1)} %bitcast.823), channel_id=1, source_target_pairs={{0,1},{1,2},{2,3},{3,4},{4,5},{5,6},{6,7},{7,8},{8,9},{9,10},{10,1... | collective-permute-start | bytes 9224 | tf_op jit(solution)/shard_map/ppermute | solution.py:41
  324.2 6.4 %collective-permute-start.28 = (f32[3,64,128]{2,1,0:T(8,128)S(1)}, f32[3,64,128]{2,1,0:T(8,128)S(1)}, u32[]{:S(2)}, u32[]{:S(2)}) collective-permute-start(f32[3,64,128]{2,1,0:T(8,128)S(1)} %fusion.278), channel_id=1, source_target_pairs={{0,16},{16,32},{32,48},{48,64},{64,80},{80,96},{96,112},{112,128},... | collective-permute-start | bytes 294920 | tf_op jit(solution)/shard_map/ppermute | solution.py:41
  328.7 6.3 %collective-permute-start.29 = (f32[4,64,128]{2,1,0:T(8,128)S(1)}, f32[4,64,128]{2,1,0:T(8,128)S(1)}, u32[]{:S(2)}, u32[]{:S(2)}) collective-permute-start(f32[4,64,128]{2,1,0:T(8,128)S(1)} %fusion.271), channel_id=1, source_target_pairs={{16,0},{32,16},{48,32},{64,48},{80,64},{96,80},{112,96},{128,112},... | collective-permute-start | bytes 393224 | tf_op jit(solution)/shard_map/ppermute | solution.py:41
  338.6 1.2 copy-start.13
  340.7 15.6 %all-to-all-start.13 = ((f32[32,1,2]{2,1,0:T(1,128)}), f32[32,1,2]{2,1,0:T(1,128)S(1)}, u32[]{:S(2)}, u32[]{:S(2)}) async-start(f32[32,1,2]{2,1,0:T(1,128)} %broadcast_in_dim.464), calls=%async_computation.13 | async-start | bytes 32768 | tf_op jit(solution)/shard_map/all_to_all | solution.py:46
  366.2 16.1 %collective-permute-start.35 = (f32[4,2,128]{2,1,0:T(2,128)S(1)}, f32[4,2,128]{2,1,0:T(2,128)S(1)}, u32[]{:S(2)}, u32[]{:S(2)}) collective-permute-start(f32[4,2,128]{2,1,0:T(2,128)S(1)} %fusion.286), channel_id=1, source_target_pairs={{1,0},{2,1},{3,2},{4,3},{5,4},{6,5},{7,6},{8,7},{9,8},{10,9},{11,1... | collective-permute-start | bytes 12296 | tf_op jit(solution)/shard_map/ppermute | solution.py:41
  367.5 14.8 %collective-permute-start.34 = (f32[3,2,128]{2,1,0:T(2,128)S(1)}, f32[3,2,128]{2,1,0:T(2,128)S(1)}, u32[]{:S(2)}, u32[]{:S(2)}) collective-permute-start(f32[3,2,128]{2,1,0:T(2,128)S(1)} %bitcast.818), channel_id=1, source_target_pairs={{0,1},{1,2},{2,3},{3,4},{4,5},{5,6},{6,7},{7,8},{8,9},{9,10},{10,1... | collective-permute-start | bytes 9224 | tf_op jit(solution)/shard_map/ppermute | solution.py:41
  371.5 6.4 %collective-permute-start.32 = (f32[3,64,128]{2,1,0:T(8,128)S(1)}, f32[3,64,128]{2,1,0:T(8,128)S(1)}, u32[]{:S(2)}, u32[]{:S(2)}) collective-permute-start(f32[3,64,128]{2,1,0:T(8,128)S(1)} %fusion.277), channel_id=1, source_target_pairs={{0,16},{16,32},{32,48},{48,64},{64,80},{80,96},{96,112},{112,128},... | collective-permute-start | bytes 294920 | tf_op jit(solution)/shard_map/ppermute | solution.py:41
  376.0 6.3 %collective-permute-start.33 = (f32[4,64,128]{2,1,0:T(8,128)S(1)}, f32[4,64,128]{2,1,0:T(8,128)S(1)}, u32[]{:S(2)}, u32[]{:S(2)}) collective-permute-start(f32[4,64,128]{2,1,0:T(8,128)S(1)} %fusion.270), channel_id=1, source_target_pairs={{16,0},{32,16},{48,32},{64,48},{80,64},{96,80},{112,96},{128,112},... | collective-permute-start | bytes 393224 | tf_op jit(solution)/shard_map/ppermute | solution.py:41
  (10 other events, 10.5 us)
where the time goes:
time: 413 us; the launch traced here: 410 us
  starting transfers between devices  157 us (38%)
  waiting for transfers between devices  118 us (29%)
  blocking collectives  101 us (24%)
  local copies, waits for them, and re-layouts  20.4 us (5%)
  other arithmetic  12.1 us (3%)
    all_to_all x9, blocking collectives, from_everyone(): lax.all_to_all(jnp.broadcast_to(array[None], (length, *array.shape)), axi...  101 us
    ppermute x32, starting transfers between devices, from_behind(): return lax.ppermute(block, axis, route)  91.9 us
    all_to_all x7, waiting for transfers between devices, from_everyone(): lax.all_to_all(jnp.broadcast_to(array[None], (length, *array.shape)), axi...  82 us
    all_to_all x7, starting transfers between devices, from_everyone(): lax.all_to_all(jnp.broadcast_to(array[None], (length, *array.shape)), axi...  40.8 us
    ppermute x32, waiting for transfers between devices, from_behind(): return lax.ppermute(block, axis, route)  27 us
    all_to_all x1, starting transfers between devices, per_device(): lax.all_to_all(jnp.where(is_bed, bed_pieces, flow_pieces), GRP_GX, split_...  11.9 us
  transfers between devices with their start and end apart: 44, of which 17 were waited for; matrix products, arithmetic and copies ran while one was open for 2% of the time, Pallas kernels for 0%

commit v1 on v0

v1 whole, which is shorter than its diff:
```python
import functools
import jax
import jax.numpy as jnp
from jax import lax
from jax.experimental import pallas as pl
from jax.experimental.pallas import tpu as pltpu
from jax.sharding import PartitionSpec as P

MESH = pl.DeviceIdType.MESH
C = 0.8 / 6.0
CC = (0.8 / 6.0) * (0.8 / 6.0)
SCALE = 1.0 / 16.0
ROWS = 96
OWN = range(2, 10)
WIDE = range(1, 11)


def loop(lo, hi, body, carry):
    for x in range(lo, hi):
        carry = body(x, carry)
    return carry


def two_sum(a, b):
    s = a + b
    bb = s - a
    return s, (a - (s - bb)) + (b - bb)


def quick(a, b):
    s = a + b
    return s, b - (s - a)


def halves(a):
    t = a * 4097.0
    hi = t - (t - a)
    return hi, a - hi


def two_prod(a, b):
    p = a * b
    ah, al = halves(a)
    bh, bl = halves(b)
    return p, ((ah * bh - p) + ah * bl + al * bh) + al * bl


def dadd(a, b):
    s, e = two_sum(a[0], b[0])
    return quick(s, e + (a[1] + b[1]))


def dsub(a, b):
    return dadd(a, (-b[0], -b[1]))


def dmul(a, b):
    p, e = two_prod(a[0], b[0])
    return quick(p, e + (a[0] * b[1] + a[1] * b[0]))


def drecip(a):
    r = 1.0 / a[0]
    p, pe = two_prod(r, a[0])
    e = ((1.0 - p) - pe) - r * a[1]
    return quick(r, r * e)


def tree(pairs):
    pairs = list(pairs)
    while len(pairs) > 1:
        nxt = []
        for i in range(0, len(pairs) - 1, 2):
            (ah, al), (bh, bl) = pairs[i], pairs[i + 1]
            s, e = two_sum(ah, bh)
            nxt.append((s, e + (al + bl)))
        if len(pairs) % 2:
            nxt.append(pairs[-1])
        pairs = nxt
    return pairs[0]


def coefficients(mu):
    n = 4
    m = [[mu[i + j + 1] for j in range(n)] for i in range(n)]
    y = [mu[i] for i in range(n)]
    low = [[None] * n for _ in range(n)]
    inv = [None] * n
    for k in range(n):
        good = m[k][k][0] > 1e-12 * mu[2 * k + 1][0]
        safe = jnp.where(good, m[k][k][0], 1.0)
        rh, rl = drecip((safe, m[k][k][1]))
        inv[k] = (jnp.where(good, rh, 0.0), jnp.where(good, rl, 0.0))
        for i in range(k + 1, n):
            low[i][k] = dmul(m[i][k], inv[k])
        for i in range(k + 1, n):
            for j in range(k + 1, i + 1):
                m[i][j] = dsub(m[i][j], dmul(low[i][k], m[j][k]))
                m[j][i] = m[i][j]
            y[i] = dsub(y[i], dmul(low[i][k], y[k]))
    c = [None] * n
    for k in range(n - 1, -1, -1):
        s = dmul(y[k], inv[k])
        for i in range(k + 1, n):
            s = dsub(s, dmul(low[i][k], c[i]))
        c[k] = s
    return [v[0] * SCALE for v in c]


def kernel(n_grp, n_gx, n_gy, drive, perm, out, fb, e2, e3, e4, tmp, kb, w, v1, v2, v3, b2, mt, zt,
           surf, spb, infl, infs, ar1, ar2,
           lsem, hs, hr, a1s, a1r, a2s, a2r, sus, sur, ins, inr):
    grp = lax.axis_index("grp")
    gx = lax.axis_index("gx")
    gy = lax.axis_index("gy")
    flows = (n_grp - 1) * n_gx
    is_bed = grp == n_grp - 1
    j = grp * n_gx + gx
    m_of = lax.div(j, 3)
    r_of = j - 3 * m_of
    lane = lax.broadcasted_iota(jnp.int32, (8, 128), 1)
    sub = lax.broadcasted_iota(jnp.int32, (8, 128), 0)
    l0 = lane == 0
    l127 = lane == 127

    def inside(i, n):
        return (i >= 0) & (i < n)

    def held(i, n):
        return jnp.minimum(jnp.maximum(i, 0), n - 1)

    def at(flow):
        flow = held(flow, flows)
        return (lax.div(flow, n_gx), lax.rem(flow, n_gx))

    def below(f):
        return jnp.where(l0, 0.0, pltpu.roll(f, 1, 1))

    def above(f):
        return jnp.where(l127, 0.0, pltpu.roll(f, 127, 1))

    barrier = pltpu.get_barrier_semaphore()
    dirs = [(dx, dy) for dx in (-1, 0, 1) for dy in (-1, 0, 1) if (dx, dy) != (0, 0)]

    def greet(partners):
        total = jnp.int32(0)
        for ok, ident in partners:
            @pl.when(ok)
            def _(ident=ident):
                pl.semaphore_signal(barrier, inc=1, device_id=ident, device_id_type=MESH)
            total = total + ok.astype(jnp.int32)
        return total

    def run(copies):
        for ok, cp in copies:
            @pl.when(ok)
            def _(cp=cp):
                cp.start()

    def arrive(copies):
        for ok, cp in copies:
            @pl.when(ok)
            def _(cp=cp):
                cp.wait_recv()

    def drain(copies):
        for ok, cp in copies:
            @pl.when(ok)
            def _(cp=cp):
                cp.wait_send()

    def remote(src, dst, s, r, ident):
        return pltpu.make_async_remote_copy(src_ref=src, dst_ref=dst, send_sem=s, recv_sem=r,
                                            device_id=ident, device_id_type=MESH)

    def halo(e, view, first, width, wide, neighbour, exists, corners):
        sends, recvs = [], []
        for dx, dy in dirs:
            if not corners and dx != 0 and dy != 0:
                continue
            if dx == 0:
                sc, dc = (first, width), (first, width)
            elif dx == 1:
                sc, dc = (first + width - wide, wide), (first - wide, wide)
            else:
                sc, dc = (first, wide), (first + width, wide)
            if dy == 0:
                sr, dr = (16, 64), (16, 64)
            elif dy == 1:
                sr, dr = (72, 8), (8, 8)
            else:
                sr, dr = (16, 8), (80, 8)
            d = (dx + 1) * 3 + dy + 1
            cp = remote(view(sc, sr), view(dc, dr), hs.at[e, d], hr.at[e, d], neighbour(dx, dy))
            sends.append((exists(dx, dy), cp))
            recvs.append((exists(-dx, -dy), remote(view(sc, sr), view(dc, dr), hs.at[e, d], hr.at[e, d],
                                                   neighbour(-dx, -dy))))
        return sends, recvs

    @pl.when(jnp.logical_not(is_bed))
    def _():
        infl[...] = jnp.zeros_like(infl)
        load = pltpu.make_async_copy(drive, fb.at[:, 2:4, 16:80, :], lsem.at[0])
        load.start()

        def neighbour(dx, dy):
            a, b = at(j + dx)
            return (a, b, held(gy + dy, n_gy))

        def exists(dx, dy):
            return inside(j + dx, flows) & inside(gy + dy, n_gy)

        beds = []
        for dm in (-1, 0, 1):
            for dy in (-1, 0, 1):
                ok = inside(m_of + dm, n_gx) & inside(gy + dy, n_gy)
                if dm == -1:
                    ok = ok & (r_of <= 1)
                if dm == 1:
                    ok = ok & (r_of >= 1)
                beds.append((dm, dy, ok, (n_grp - 1, held(m_of + dm, n_gx), held(gy + dy, n_gy))))

        total = greet([(exists(dx, dy), neighbour(dx, dy)) for dx, dy in dirs]
                      + [(ok, ident) for _, _, ok, ident in beds])

        def clear(c0, c1, r0, r1):
            for buf in (fb, e2, e3, e4):
                buf[:, c0:c1, r0:r1, :] = jnp.zeros((buf.shape[0], c1 - c0, r1 - r0, 128), jnp.float32)

        @pl.when(j == 0)
        def _():
            clear(0, 2, 8, 88)

        @pl.when(j == flows - 1)
        def _():
            clear(4, 6, 8, 88)

        @pl.when(gy == 0)
        def _():
            clear(0, 6, 8, 16)

        @pl.when(gy == n_gy - 1)
        def _():
            clear(0, 6, 80, 88)

        pl.semaphore_wait(barrier, total)
        load.wait()

        def exchange(e, buf, wide, corners):
            view = lambda c, r: buf.at[:, pl.ds(*c), pl.ds(*r), :]
            sends, recvs = halo(e, view, 2, 2, wide, neighbour, exists, corners)
            run(sends)
            arrive(recvs)
            return sends

        pending = exchange(0, fb, 2, True)

        def valid(x, t):
            ok = inside(j * 2 + x - 2, 2 * flows)
            if t == 1:
                ok = ok & (gy > 0)
            if t == 10:
                ok = ok & (gy < n_gy - 1)
            return ok

        def near(src, f, x, r):
            return (src[f, x - 1, pl.ds(r, 8), :], src[f, x + 1, pl.ds(r, 8), :],
                    src[f, x, pl.ds(r - 1, 8), :], src[f, x, pl.ds(r + 1, 8), :])

        def first_sweep(dst, cols, tiles):
            def body(x, _):
                for t in tiles:
                    r = 8 * t
                    div = None
                    for f in range(3):
                        c = fb[f, x, pl.ds(r, 8), :]
                        we, ea, so, no = near(fb, f, x, r)
                        be = below(c)
                        total = ((we + ea) + (so + no)) + (be + above(c))
                        dst[f, x, pl.ds(r, 8), :] = jnp.where(valid(x, t), (1.2 * C) * c + CC * total, 0.0)
                        part = c - (we, so, be)[f]
                        div = part if div is None else div + part
                    dst[3, x, pl.ds(r, 8), :] = jnp.where(valid(x, t), (-0.5 * C) * div, 0.0)
                return 0
            loop(cols[0], cols[1], body, 0)

        def sweep(src, put, cols, tiles, masked):
            def body(x, _):
                for t in tiles:
                    r = 8 * t
                    p = src[3, x, pl.ds(r, 8), :]
                    toward = (src[3, x + 1, pl.ds(r, 8), :], src[3, x, pl.ds(r + 1, 8), :], above(p))
                    div = None
                    for f in range(3):
                        c = src[f, x, pl.ds(r, 8), :]
                        we, ea, so, no = near(src, f, x, r)
                        be = below(c)
                        total = ((we + ea) + (so + no)) + (be + above(c))
                        total = total + (fb[f, x, pl.ds(r, 8), :] - (toward[f] - p))
                        new = 0.2 * c + C * total
                        put(f, x, r, jnp.where(valid(x, t), new, 0.0) if masked else new)
                        part = c - (we, so, be)[f]
                        div = part if div is None else div + part
                    new = p - 0.5 * div
                    put(3, x, r, jnp.where(valid(x, t), new, 0.0) if masked else new)
                return 0
            loop(cols[0], cols[1], body, 0)

        def into(buf):
            def put(f, x, r, value):
                buf[f, x, pl.ds(r, 8), :] = value
            return put

        def final(f, x, r, value):
            if f < 3:
                out[f, x - 2, pl.ds(r - 16, 8), :] = value

        first_sweep(tmp, (1, 5), WIDE)
        sweep(tmp, into(e2), (2, 4), OWN, False)
        pending += exchange(1, e2, 1, False)
        sweep(e2, into(e3), (2, 4), OWN, False)

        view = lambda c, r: e3.at[:, pl.ds(*c), pl.ds(*r), :]
        sends3, recvs3 = halo(2, view, 2, 2, 2, neighbour, exists, True)
        run(sends3)
        plane = jnp.concatenate([e3[3, 2, 16:80, :], e3[3, 3, 16:80, :]], axis=0)
        spb[8] = plane.T[0:1, :]
        tells = []
        for dm, dy, ok, ident in beds:
            for r in range(3):
                slot = r + 2 - 3 * dm
                if 0 <= slot < 7:
                    tells.append((ok & (r_of == r), remote(spb.at[8], surf.at[1 - dy, slot], sus.at[1 - dy, slot],
                                                           sur.at[1 - dy, slot], ident)))
        run(tells)
        arrive(recvs3)
        pending += sends3 + tells
        sweep(e3, into(tmp), (1, 5), WIDE, True)
        sweep(tmp, into(e4), (2, 4), OWN, False)
        pending += exchange(3, e4, 2, True)
        sweep(e4, into(tmp), (1, 5), WIDE, True)
        sweep(tmp, final, (2, 4), OWN, False)

        for dm, dy, ok, ident in beds:
            @pl.when(ok)
            def _(dm=dm, dy=dy, ident=ident):
                remote(infs.at[8:11], infl.at[1 + dy, dm + 1], ins.at[0], inr.at[1 + dy, dm + 1], ident).wait_recv()
        even = lax.rem(sub, 2) == 0
        rows = []
        for s in range(3):
            parts = []
            for o in range(-2, 3):
                pick = [jnp.broadcast_to(infl[s, (r + o + 3) // 3, (r + o + 3) % 3], (8, 128)) for r in range(3)]
                parts.append(jnp.where(r_of == 0, pick[0], jnp.where(r_of == 1, pick[1], pick[2])))
            a = parts[0]
            for k in range(1, 5):
                a = jnp.where(sub >= 2 * k - 1, parts[k], a)
            rows.append((pltpu.roll(a, 32, 1), pltpu.roll(a, 96, 1)))
        middle = jnp.where(even, rows[1][1], rows[1][0])
        south = jnp.where(even, rows[0][0], rows[0][1])
        north = jnp.where(even, rows[2][0], rows[2][1])
        column = j * 2 - 3 + sub
        live = (column >= 0) & (column < 2 * flows)
        live = live & ((lane >= 32) | (gy > 0)) & ((lane < 96) | (gy < n_gy - 1))
        inflow = jnp.where(lane < 32, south, jnp.where(lane < 96, middle, north))
        inflow = jnp.where(live, inflow, 0.0)

        def plus(a, b):
            return b if a is None else (a if b is None else a + b)

        def minus(a, b):
            return a if b is None else (-b if a is None else a - b)

        def side(a, k):
            if a is None:
                return None
            return (pltpu.roll(a, 1, 0), pltpu.roll(a, 7, 0), pltpu.roll(a, 1, 1), pltpu.roll(a, 127, 1))[k]

        fields = [[None] * 6 for _ in range(4)]
        for step in range(4):
            new = [[None] * 6 for _ in range(4)]
            for z in range(step + 1):
                div = None
                for f in range(3):
                    c = fields[f][z]
                    if z > 0:
                        be = fields[f][z - 1]
                    else:
                        be = inflow if f == 2 else None
                    sides = [side(c, k) for k in range(4)]
                    total = plus(be, fields[f][z + 1])
                    for k in range(4):
                        total = plus(total, sides[k])
                    p = fields[3][z]
                    ahead = (side(p, 1), side(p, 3), fields[3][z + 1])[f]
                    total = plus(minus(total, ahead), p)
                    value = None if total is None else C * total
                    if c is not None:
                        value = plus(value, 0.2 * c)
                    new[f][z] = value
                    div = plus(div, minus(c, (sides[0], sides[2], be)[f]))
                if step < 3:
                    value = fields[3][z]
                    if div is not None:
                        value = minus(value, 0.5 * div)
                    new[3][z] = value
            for f in range(4):
                for z in range(step + 1):
                    if new[f][z] is not None:
                        new[f][z] = jnp.where(live, new[f][z], 0.0)
            fields = new
        stack = []
        for f in range(3):
            for c in range(2):
                acc = jnp.zeros((8, 128), jnp.float32)
                for z in range(4):
                    if fields[f][z] is not None:
                        acc = jnp.where(sub == z, pltpu.roll(fields[f][z], (z - 3 - c) % 8, 0), acc)
                stack.append(acc)
        stack.append(jnp.zeros((80, 128), jnp.float32))
        mt[...] = jnp.concatenate(stack, axis=0).T
        for t in range(8):
            turn = mt[32 + 8 * t:40 + 8 * t, :]
            for f in range(3):
                for c in range(2):
                    add = pltpu.roll(turn, (128 - 8 * (2 * f + c)) % 128, 1)
                    out[f, c, 8 * t:8 * t + 8, :] += jnp.where(lane < 8, add, 0.0)
        drain(pending)

    @pl.when(is_bed)
    def _():
        surf[...] = jnp.zeros_like(surf)
        loads = [pltpu.make_async_copy(perm, kb.at[0, 4:10, 16:80, :], lsem.at[0])]
        for c in range(3):
            loads.append(pltpu.make_async_copy(drive.at[c], kb.at[1, 4 + 2 * c:6 + 2 * c, 16:80, :], lsem.at[1 + c]))
        for cp in loads:
            cp.start()

        def neighbour(dx, dy):
            return (n_grp - 1, held(gx + dx, n_gx), held(gy + dy, n_gy))

        def exists(dx, dy):
            return inside(gx + dx, n_gx) & inside(gy + dy, n_gy)

        always = grp >= 0
        over_x = [(d, (n_grp - 1, lax.rem(gx + d, n_gx), gy)) for d in range(1, n_gx)]
        over_y = [(d, (n_grp - 1, gx, lax.rem(gy + d, n_gy))) for d in range(1, n_gy)]
        mates = []
        for k in range(7):
            flow = 3 * gx - 2 + k
            for dy in (-1, 0, 1):
                a, b = at(flow)
                mates.append((k, dy, inside(flow, flows) & inside(gy + dy, n_gy), (a, b, held(gy + dy, n_gy))))
        total = greet([(exists(dx, dy), neighbour(dx, dy)) for dx, dy in dirs]
                      + [(always, ident) for _, ident in over_x + over_y]
                      + [(ok, ident) for _, _, ok, ident in mates])

        def clear(c0, c1, r0, r1):
            kb[:, c0:c1, r0:r1, :] = jnp.zeros((2, c1 - c0, r1 - r0, 128), jnp.float32)

        @pl.when(gx == 0)
        def _():
            clear(0, 4, 8, 88)

        @pl.when(gx == n_gx - 1)
        def _():
            clear(10, 14, 8, 88)

        @pl.when(gy == 0)
        def _():
            clear(0, 14, 8, 16)

        @pl.when(gy == n_gy - 1)
        def _():
            clear(0, 14, 80, 88)

        pl.semaphore_wait(barrier, total)
        for cp in loads:
            cp.wait()
        view = lambda c, r: kb.at[:, pl.ds(*c), pl.ds(*r), :]
        pending, recvs = halo(4, view, 4, 6, 4, neighbour, exists, True)
        run(pending)
        arrive(recvs)

        def weight(x, _):
            open_x = gx >= 0
            if x == 3:
                open_x = gx > 0
            if x == 9:
                open_x = gx < n_gx - 1
            for t in WIDE:
                r = 8 * t
                k = kb[0, x, pl.ds(r, 8), :]
                w[0, x, pl.ds(r, 8), :] = jnp.where(open_x, (k + kb[0, x + 1, pl.ds(r, 8), :]) * (0.5 * SCALE), 0.0)
                wy = (k + kb[0, x, pl.ds(r + 1, 8), :]) * (0.5 * SCALE)
                if t == 1:
                    wy = jnp.where((gy == 0) & (sub == 7), 0.0, wy)
                if t == 9:
                    wy = jnp.where((gy == n_gy - 1) & (sub == 7), 0.0, wy)
                w[1, x, pl.ds(r, 8), :] = wy
                up = pltpu.roll(k, 127, 1)
                w[2, x, pl.ds(r, 8), :] = jnp.where(l127, k * SCALE, (k + up) * (0.5 * SCALE))
            return 0

        loop(0, 13, weight, 0)

        def image(src, x, t):
            r = 8 * t
            f = src(x, r)
            ge = w[0, x, pl.ds(r, 8), :] * (f - src(x + 1, r))
            gw = w[0, x - 1, pl.ds(r, 8), :] * (f - src(x - 1, r))
            gn = w[1, x, pl.ds(r, 8), :] * (f - src(x, r + 1))
            gs = w[1, x, pl.ds(r - 1, 8), :] * (f - src(x, r - 1))
            gz = w[2, x, pl.ds(r, 8), :] * (f - above(f))
            return ((ge + gw) + (gn + gs)) + (gz - below(gz))

        def reader(ref):
            return lambda x, r: ref[x, pl.ds(r, 8), :]

        r1, r2, r3 = reader(v1), reader(v2), reader(v3)

        def powers(src):
            for here, there, lo, hi in ((src, v1, 1, 13), (r1, v2, 2, 12), (r2, v3, 3, 11)):
                def body(x, _, here=here, there=there):
                    for t in WIDE:
                        there[x, pl.ds(8 * t, 8), :] = image(here, x, t)
                    return 0
                loop(lo, hi, body, 0)

            def body(x, acc):
                acc = list(acc)
                for t in OWN:
                    v = [get(x, 8 * t) for get in (src, r1, r2, r3)] + [image(r3, x, t)]
                    for i in range(8):
                        s, e = two_sum(acc[2 * i], v[i // 2] * v[(i + 1) // 2])
                        acc[2 * i] = s
                        acc[2 * i + 1] = acc[2 * i + 1] + e
                return tuple(acc)
            acc = loop(4, 10, body, tuple(jnp.zeros((8, 128), jnp.float32) for _ in range(16)))
            level = [(acc[2 * i], acc[2 * i + 1]) for i in range(8)]
            for d in (4, 2, 1):
                keep = (sub & d) == 0
                nxt = []
                for i in range(d):
                    a, b = level[i], level[i + d]
                    x = [jnp.where(keep, a[h], b[h]) for h in range(2)]
                    y = [jnp.where(keep, b[h], a[h]) for h in range(2)]
                    y = [jnp.where(keep, pltpu.roll(q, 8 - d, 0), pltpu.roll(q, d, 0)) for q in y]
                    s, e = two_sum(x[0], y[0])
                    nxt.append((s, e + (x[1] + y[1])))
                level = nxt
            return level[0]

        def spread_x(s, pair):
            ar1[s, 0, 0] = pair[0]
            ar1[s, 0, 1] = pair[1]
            cps = [(always, remote(ar1.at[s, 0], ar1.at[s, d], a1s.at[s, d], a1r.at[s, d], ident)) for d, ident in over_x]
            run(cps)
            return cps

        def spread_y(s, cps):
            arrive(cps)
            hi, lo = tree((ar1[s, d, 0], ar1[s, d, 1]) for d in range(n_gx))
            big = jnp.max(jnp.abs(hi), axis=1, keepdims=True) * 512.0
            top = (hi + big) - big
            th = jnp.sum(top, axis=1, keepdims=True)
            tl = jnp.sum((hi - top) + lo, axis=1, keepdims=True)
            th, tl = two_sum(th, tl)
            spot = jnp.where(lane == sub, th, jnp.where(lane == sub + 8, tl, 0.0))
            ar2[s, 8] = jnp.sum(spot, axis=0, keepdims=True)
            out_cps = [(always, remote(ar2.at[s, 8], ar2.at[s, 8 + d], a2s.at[s, d], a2r.at[s, d], ident)) for d, ident in over_y]
            run(out_cps)
            return out_cps

        def solve(s, cps):
            arrive(cps)
            hi, lo = tree((ar2[s, 8 + d], jnp.zeros((1, 128), jnp.float32)) for d in range(n_gy))
            hi = jnp.broadcast_to(hi, (8, 128))
            lo = jnp.broadcast_to(lo, (8, 128))
            th = jnp.sum(jnp.where(lane == sub, hi, 0.0), axis=1, keepdims=True)
            tl = jnp.sum(jnp.where(lane == sub, lo, jnp.where(lane == sub + 8, hi, 0.0)), axis=1, keepdims=True)
            th = jnp.broadcast_to(th, (8, 128))
            tl = jnp.broadcast_to(tl, (8, 128))
            mu = [quick(jnp.broadcast_to(th[i:i + 1], (8, 128)), jnp.broadcast_to(tl[i:i + 1], (8, 128))) for i in range(8)]
            return coefficients(mu)

        def source(x, r):
            return kb[1, x, pl.ds(r, 8), :]

        first_x = spread_x(0, powers(source))

        tiles = []
        for c in range(2):
            for t in OWN:
                acc = jnp.zeros((8, 128), jnp.float32)
                for q in range(3):
                    x = 4 + 2 * q + c
                    k = kb[0, x, pl.ds(8 * t, 8), :]
                    for i, get in enumerate((source, r1, r2, r3)):
                        at_lane = i * 8 + q
                        acc = jnp.where(lane == at_lane, pltpu.roll(k * get(x, 8 * t), at_lane + 1, 1), acc)
                tiles.append(acc)
        zt[...] = jnp.concatenate(tiles, axis=0).T[0:32, :]

        first_y = spread_y(0, first_x)

        for k, dy, ok, ident in mates:
            @pl.when(ok)
            def _(k=k, dy=dy, ident=ident):
                remote(spb.at[8], surf.at[1 + dy, k], sus.at[0, 0], sur.at[1 + dy, k], ident).wait_recv()
        rows = []
        for s in range(3):
            a = jnp.zeros((8, 128), jnp.float32)
            for k in range(7):
                a = jnp.where(sub == k, jnp.broadcast_to(surf[s, k], (8, 128)), a)
            rows.append(a)
        rows.append(jnp.zeros((104, 128), jnp.float32))
        mt[...] = jnp.concatenate(rows, axis=0).T
        for k in range(7):
            for c in range(2):
                x = 2 * k + c
                for t in WIDE:
                    if t == 1:
                        r, at_lane = c * 64 + 56, k
                    elif t == 10:
                        r, at_lane = c * 64, 16 + k
                    else:
                        r, at_lane = c * 64 + 8 * (t - 2), 8 + k
                    p = pltpu.roll(mt[r:r + 8, :], 127 - at_lane, 1)
                    k8 = kb[0, x, pl.ds(8 * t, 8), :]
                    b2[x, pl.ds(8 * t, 8), :] = kb[1, x, pl.ds(8 * t, 8), :] + jnp.where(l127, k8 * (0.5 * p), 0.0)

        second_x = spread_x(1, powers(reader(b2)))
        second_y = spread_y(1, second_x)
        c1 = solve(0, first_y)
        flow_in = c1[0] * zt[0:8, :]
        for i in range(1, 4):
            flow_in = flow_in + c1[i] * zt[8 * i:8 * i + 8, :]
        for q in range(3):
            infs[8 + q] = flow_in[q:q + 1, :]
        tells = []
        for k, dy, ok, ident in mates:
            dm = (1, 1, 0, 0, 0, -1, -1)[k]
            tells.append((ok, remote(infs.at[8:11], infl.at[1 - dy, dm + 1], ins.at[k * 3 + dy + 1], inr.at[1 - dy, dm + 1], ident)))
        run(tells)
        c2 = solve(1, second_y)

        for x in range(4, 10):
            for t in OWN:
                rows8 = pl.ds(8 * t, 8)
                total = (c2[0] * b2[x, rows8, :] + c2[1] * v1[x, rows8, :]) + (c2[2] * v2[x, rows8, :] + c2[3] * v3[x, rows8, :])
                out[(x - 4) // 2, x % 2, pl.ds(8 * t - 16, 8), :] = total
        drain(pending + first_x + first_y + second_x + second_y + tells)


def solution(mesh):
    n_grp, n_gx, n_gy = mesh.shape["grp"], mesh.shape["gx"], mesh.shape["gy"]

    def per_device(drive, permeability):
        vmem = lambda *shape: pltpu.VMEM(shape, jnp.float32)
        dma = lambda *shape: pltpu.SemaphoreType.DMA(shape)
        return pl.pallas_call(
            functools.partial(kernel, n_grp, n_gx, n_gy),
            out_shape=jax.ShapeDtypeStruct(drive.shape, jnp.float32),
            in_specs=[pl.BlockSpec(memory_space=pl.ANY)] * 2,
            out_specs=pl.BlockSpec(memory_space=pltpu.VMEM),
            scratch_shapes=[
                vmem(3, 6, ROWS, 128), vmem(4, 6, ROWS, 128), vmem(4, 6, ROWS, 128),
                vmem(4, 6, ROWS, 128), vmem(4, 6, ROWS, 128),
                vmem(2, 14, ROWS, 128), vmem(3, 14, ROWS, 128),
                vmem(14, ROWS, 128), vmem(14, ROWS, 128), vmem(14, ROWS, 128), vmem(14, ROWS, 128),
                vmem(128, 128), vmem(32, 128),
                vmem(4, 8, 1, 128), vmem(24, 1, 128), vmem(4, 3, 3, 1, 128), vmem(24, 1, 128),
                vmem(2, 8, 2, 8, 128), vmem(2, 32, 1, 128),
                dma(4), dma(5, 9), dma(5, 9), dma(2, 8), dma(2, 8), dma(2, 16), dma(2, 16),
                dma(3, 7), dma(3, 7), dma(21), dma(3, 3),
            ],
            compiler_params=pltpu.CompilerParams(collective_id=0, has_side_effects=True, vmem_limit_bytes=40 * 1024 * 1024),
            name="coupling",
        )(drive, permeability)

    return jax.shard_map(
        per_device,
        mesh=mesh,
        in_specs=(P(None, ("grp", "gx"), "gy", None), P("gx", "gy", None)),
        out_specs=P(None, ("grp", "gx"), "gy", None),
        check_vma=False,
    )
```

time: 413 us -> 49.4 us (0.12)
  the two profiles are of different devices: /device:TPU:1 before, /device:TPU:6 now
where the time goes in v1:
time: 49.4 us; the launch traced here: 49.3 us
  Pallas kernels  46.7 us (95%)
  local copies, waits for them, and re-layouts  2.53 us (5%)
    pallas_call x1, Pallas kernels, per_device(): pl.pallas_call(functools.partial(kernel, n_grp, n_gx, n_gy), out_shape=ja...  46.7 us
    unnamed x5, local copies, waits for them, and re-layouts  2.53 us

profile of v1, /device:TPU:6, one launch (start us, length us, event | category | flops | bytes accessed | tf_op | source)
XLA Modules:
  0.0 49.3 jit_solution(2686857873534783635)
XLA Ops:
  0.0 0.0 copy-start
  0.0 0.9 %copy-done = f32[3,2,64,128]{3,2,1,0:T(8,128)S(1)} copy-done((f32[3,2,64,128]{3,2,1,0:T(8,128)S(1)}, f32[3,2,64,128]{3,2,1,0:T(8,128)}, u32[]{:S(2)}) %copy-start) | copy-done | bytes 196632
  0.9 0.0 copy-start.1
  0.9 0.9 %copy-done.1 = f32[6,64,128]{2,1,0:T(8,128)S(1)} copy-done((f32[6,64,128]{2,1,0:T(8,128)S(1)}, f32[6,64,128]{2,1,0:T(8,128)}, u32[]{:S(2)}) %copy-start.1) | copy-done | bytes 196632
  1.9 46.7 %coupling.1 = f32[3,2,64,128]{3,2,1,0:T(8,128)S(1)} custom-call(f32[3,2,64,128]{3,2,1,0:T(8,128)S(1)} %copy-done, f32[6,64,128]{2,1,0:T(8,128)S(1)} %copy-done.1), custom_call_target="tpu_custom_call" | custom-call | tf_op jit(solution)/shard_map/coupling/pallas_call | solution.py:662
  48.6 0.7 %copy.4 = f32[3,2,64,128]{3,2,1,0:T(8,128)} copy(f32[3,2,64,128]{3,2,1,0:T(8,128)S(1)} %coupling.1) | data formatting | bytes 393216
Async XLA Ops:
  0.0 0.9 %copy-start = (f32[3,2,64,128]{3,2,1,0:T(8,128)S(1)}, f32[3,2,64,128]{3,2,1,0:T(8,128)}, u32[]{:S(2)}) copy-start(f32[3,2,64,128]{3,2,1,0:T(8,128)} %drive.1) | copy-start | bytes 589828
  0.9 0.9 %copy-start.1 = (f32[6,64,128]{2,1,0:T(8,128)S(1)}, f32[6,64,128]{2,1,0:T(8,128)}, u32[]{:S(2)}) copy-start(f32[6,64,128]{2,1,0:T(8,128)} %perm.1) | copy-start | bytes 589828

commit v2 on v1

--- a/solution.py
+++ b/solution.py
@@ -108,8 +108,8 @@
 
 
 def kernel(n_grp, n_gx, n_gy, drive, perm, out, fb, e2, e3, e4, tmp, kb, w, v1, v2, v3, b2, mt, zt,
-           surf, spb, infl, infs, ar1, ar2,
-           lsem, hs, hr, a1s, a1r, a2s, a2r, sus, sur, ins, inr):
+           surf, spb, infl, infs, ar1, ar2, nb, nbs,
+           lsem, hs, hr, a1s, a1r, a2s, a2r, sus, sur, ins, inr, ns, nr, tok, ready):
     grp = lax.axis_index("grp")
     gx = lax.axis_index("gx")
     gy = lax.axis_index("gy")
@@ -200,6 +200,7 @@
     @pl.when(jnp.logical_not(is_bed))
     def _():
         infl[...] = jnp.zeros_like(infl)
+        nb[...] = jnp.zeros_like(nb)
         load = pltpu.make_async_copy(drive, fb.at[:, 2:4, 16:80, :], lsem.at[0])
         load.start()
 
@@ -220,8 +221,9 @@
                     ok = ok & (r_of >= 1)
                 beds.append((dm, dy, ok, (n_grp - 1, held(m_of + dm, n_gx), held(gy + dy, n_gy))))
 
-        total = greet([(exists(dx, dy), neighbour(dx, dy)) for dx, dy in dirs]
-                      + [(ok, ident) for _, _, ok, ident in beds])
+        around = [(o, dy) for o in range(-2, 3) for dy in (-1, 0, 1) if (o, dy) != (0, 0)]
+        total = greet([(exists(o, dy), neighbour(o, dy)) for o, dy in around])
+        greet([(ok, ident) for _, _, ok, ident in beds])
 
         def clear(c0, c1, r0, r1):
             for buf in (fb, e2, e3, e4):
@@ -243,17 +245,131 @@
         def _():
             clear(0, 6, 80, 88)
 
+        load.wait()
+
+        tiles = []
+        for c in range(2):
+            for t in OWN:
+                acc = fb[0, 2 + c, 8 * t:8 * t + 8, :]
+                for f in (1, 2):
+                    acc = jnp.where(lane >= 3 * f, pltpu.roll(fb[f, 2 + c, 8 * t:8 * t + 8, :], 3 * f, 1), acc)
+                tiles.append(acc)
+        turned = jnp.concatenate(tiles, axis=0).T
+        for q in range(9):
+            nbs[8 + q] = turned[q:q + 1, :]
         pl.semaphore_wait(barrier, total)
-        load.wait()
-
-        def exchange(e, buf, wide, corners):
+        low_out, low_in = [], []
+        for o, dy in around:
+            low_out.append((exists(o, dy), remote(nbs.at[8:17], nb.at[1 - dy, 2 - o], ns.at[dy + 1, o + 2],
+                                                  nr.at[1 - dy, 2 - o], neighbour(o, dy))))
+            low_in.append((exists(o, dy), remote(nbs.at[8:17], nb.at[1 + dy, 2 + o], ns.at[dy + 1, o + 2],
+                                                 nr.at[1 + dy, 2 + o], neighbour(o, dy))))
+        run(low_out)
+
+        def begin(e, buf, wide, corners):
             view = lambda c, r: buf.at[:, pl.ds(*c), pl.ds(*r), :]
             sends, recvs = halo(e, view, 2, 2, wide, neighbour, exists, corners)
             run(sends)
+            return sends, recvs
+
+        def exchange(e, buf, wide, corners):
+            sends, recvs = begin(e, buf, wide, corners)
             arrive(recvs)
             return sends
 
-        pending = exchange(0, fb, 2, True)
+        pending, recvs0 = begin(0, fb, 2, True)
+        pending = pending + low_out
+
+        even = lax.rem(sub, 2) == 0
+        column = j * 2 - 3 + sub
+        live = (column >= 0) & (column < 2 * flows)
+        live = live & ((lane >= 32) | (gy > 0)) & ((lane < 96) | (gy < n_gy - 1))
+
+        def assemble(row):
+            rows = []
+            for i in range(3):
+                a = row(i, -2)
+                for o in range(-1, 3):
+                    a = jnp.where(sub >= 2 * o + 3, row(i, o), a)
+                rows.append((pltpu.roll(a, 32, 1), pltpu.roll(a, 96, 1)))
+            middle = jnp.where(even, rows[1][1], rows[1][0])
+            south = jnp.where(even, rows[0][0], rows[0][1])
+            north = jnp.where(even, rows[2][0], rows[2][1])
+            whole = jnp.where(lane < 32, south, jnp.where(lane < 96, middle, north))
+            return jnp.where(live, whole, 0.0)
+
+        def plus(a, b):
+            return b if a is None else (a if b is None else a + b)
+
+        def minus(a, b):
+            return a if b is None else (-b if a is None else a - b)
+
+        def side(a, k):
+            if a is None:
+                return None
+            return (pltpu.roll(a, 1, 0), pltpu.roll(a, 7, 0), pltpu.roll(a, 1, 1), pltpu.roll(a, 127, 1))[k]
+
+        def evolve(fields, inflow, force, n_velocity, n_pressure):
+            new = [[None] * 6 for _ in range(4)]
+            for z in range(max(n_velocity, n_pressure)):
+                div = None
+                for f in range(3):
+                    c = fields[f][z]
+                    if z > 0:
+                        be = fields[f][z - 1]
+                    else:
+                        be = inflow if f == 2 else None
+                    sides = [side(c, k) for k in range(4)]
+                    if z < n_velocity:
+                        total = plus(plus(be, fields[f][z + 1]), force[f][z])
+                        for k in range(4):
+                            total = plus(total, sides[k])
+                        p = fields[3][z]
+                        ahead = (side(p, 1), side(p, 3), fields[3][z + 1])[f]
+                        total = plus(minus(total, ahead), p)
+                        value = None if total is None else C * total
+                        if c is not None:
+                            value = plus(value, 0.2 * c)
+                        if value is not None:
+                            new[f][z] = jnp.where(live, value, 0.0)
+                    div = plus(div, minus(c, (sides[0], sides[2], be)[f]))
+                if z < n_pressure:
+                    value = fields[3][z]
+                    if div is not None:
+                        value = minus(value, 0.5 * div)
+                    if value is not None:
+                        new[3][z] = jnp.where(live, value, 0.0)
+            return new
+
+        nothing = [[None] * 6 for _ in range(4)]
+        arrive(low_in)
+        force = [[None] * 6 for _ in range(3)]
+        for f in range(3):
+            for z in range(3):
+                q = 3 * f + z
+
+                def row(i, o, q=q):
+                    one = nbs[8 + q] if (i, o) == (1, 0) else nb[i, o + 2, q]
+                    return jnp.broadcast_to(one, (8, 128))
+                force[f][z] = assemble(row)
+        low = evolve(nothing, None, force, 3, 0)
+        low = evolve(low, None, force, 2, 2)
+        low = evolve(low, None, force, 1, 1)
+        low = evolve(low, None, force, 0, 1)[3][0]
+        spb[8] = jnp.where(lane[0:1] < 64, pltpu.roll(low, 96, 1)[3:4], pltpu.roll(low, 32, 1)[4:5])
+        tells = []
+        for dm, dy, ok, ident in beds:
+            @pl.when(ok)
+            def _(dm=dm, dy=dy):
+                pl.semaphore_wait(ready.at[1 + dy, dm + 1], 1)
+            for r in range(3):
+                slot = r + 2 - 3 * dm
+                if 0 <= slot < 7:
+                    tells.append((ok & (r_of == r), remote(spb.at[8], surf.at[1 - dy, slot], sus.at[1 - dy, slot],
+                                                           sur.at[1 - dy, slot], ident)))
+        run(tells)
+        pending = pending + tells
+        arrive(recvs0)
 
         def valid(x, t):
             ok = inside(j * 2 + x - 2, 2 * flows)
@@ -320,21 +436,7 @@
         pending += exchange(1, e2, 1, False)
         sweep(e2, into(e3), (2, 4), OWN, False)
 
-        view = lambda c, r: e3.at[:, pl.ds(*c), pl.ds(*r), :]
-        sends3, recvs3 = halo(2, view, 2, 2, 2, neighbour, exists, True)
-        run(sends3)
-        plane = jnp.concatenate([e3[3, 2, 16:80, :], e3[3, 3, 16:80, :]], axis=0)
-        spb[8] = plane.T[0:1, :]
-        tells = []
-        for dm, dy, ok, ident in beds:
-            for r in range(3):
-                slot = r + 2 - 3 * dm
-                if 0 <= slot < 7:
-                    tells.append((ok & (r_of == r), remote(spb.at[8], surf.at[1 - dy, slot], sus.at[1 - dy, slot],
-                                                           sur.at[1 - dy, slot], ident)))
-        run(tells)
-        arrive(recvs3)
-        pending += sends3 + tells
+        pending += exchange(2, e3, 2, True)
         sweep(e3, into(tmp), (1, 5), WIDE, True)
         sweep(tmp, into(e4), (2, 4), OWN, False)
         pending += exchange(3, e4, 2, True)
@@ -345,70 +447,15 @@
             @pl.when(ok)
             def _(dm=dm, dy=dy, ident=ident):
                 remote(infs.at[8:11], infl.at[1 + dy, dm + 1], ins.at[0], inr.at[1 + dy, dm + 1], ident).wait_recv()
-        even = lax.rem(sub, 2) == 0
-        rows = []
-        for s in range(3):
-            parts = []
-            for o in range(-2, 3):
-                pick = [jnp.broadcast_to(infl[s, (r + o + 3) // 3, (r + o + 3) % 3], (8, 128)) for r in range(3)]
-                parts.append(jnp.where(r_of == 0, pick[0], jnp.where(r_of == 1, pick[1], pick[2])))
-            a = parts[0]
-            for k in range(1, 5):
-                a = jnp.where(sub >= 2 * k - 1, parts[k], a)
-            rows.append((pltpu.roll(a, 32, 1), pltpu.roll(a, 96, 1)))
-        middle = jnp.where(even, rows[1][1], rows[1][0])
-        south = jnp.where(even, rows[0][0], rows[0][1])
-        north = jnp.where(even, rows[2][0], rows[2][1])
-        column = j * 2 - 3 + sub
-        live = (column >= 0) & (column < 2 * flows)
-        live = live & ((lane >= 32) | (gy > 0)) & ((lane < 96) | (gy < n_gy - 1))
-        inflow = jnp.where(lane < 32, south, jnp.where(lane < 96, middle, north))
-        inflow = jnp.where(live, inflow, 0.0)
-
-        def plus(a, b):
-            return b if a is None else (a if b is None else a + b)
-
-        def minus(a, b):
-            return a if b is None else (-b if a is None else a - b)
-
-        def side(a, k):
-            if a is None:
-                return None
-            return (pltpu.roll(a, 1, 0), pltpu.roll(a, 7, 0), pltpu.roll(a, 1, 1), pltpu.roll(a, 127, 1))[k]
-
-        fields = [[None] * 6 for _ in range(4)]
+
+        def row(i, o):
+            pick = [jnp.broadcast_to(infl[i, (r + o + 3) // 3, (r + o + 3) % 3], (8, 128)) for r in range(3)]
+            return jnp.where(r_of == 0, pick[0], jnp.where(r_of == 1, pick[1], pick[2]))
+
+        inflow = assemble(row)
+        fields = nothing
         for step in range(4):
-            new = [[None] * 6 for _ in range(4)]
-            for z in range(step + 1):
-                div = None
-                for f in range(3):
-                    c = fields[f][z]
-                    if z > 0:
-                        be = fields[f][z - 1]
-                    else:
-                        be = inflow if f == 2 else None
-                    sides = [side(c, k) for k in range(4)]
-                    total = plus(be, fields[f][z + 1])
-                    for k in range(4):
-                        total = plus(total, sides[k])
-                    p = fields[3][z]
-                    ahead = (side(p, 1), side(p, 3), fields[3][z + 1])[f]
-                    total = plus(minus(total, ahead), p)
-                    value = None if total is None else C * total
-                    if c is not None:
-                        value = plus(value, 0.2 * c)
-                    new[f][z] = value
-                    div = plus(div, minus(c, (sides[0], sides[2], be)[f]))
-                if step < 3:
-                    value = fields[3][z]
-                    if div is not None:
-                        value = minus(value, 0.5 * div)
-                    new[3][z] = value
-            for f in range(4):
-                for z in range(step + 1):
-                    if new[f][z] is not None:
-                        new[f][z] = jnp.where(live, new[f][z], 0.0)
-            fields = new
+            fields = evolve(fields, inflow, nothing, step + 1, step + 1 if step < 3 else 0)
         stack = []
         for f in range(3):
             for c in range(2):
@@ -443,6 +490,10 @@
             return inside(gx + dx, n_gx) & inside(gy + dy, n_gy)
 
         always = grp >= 0
+
+        def ring(d):
+            return (n_grp - 1, gx, lax.rem(gy + d + n_gy, n_gy))
+
         over_x = [(d, (n_grp - 1, lax.rem(gx + d, n_gx), gy)) for d in range(1, n_gx)]
         over_y = [(d, (n_grp - 1, gx, lax.rem(gy + d, n_gy))) for d in range(1, n_gy)]
         mates = []
@@ -452,8 +503,10 @@
                 a, b = at(flow)
                 mates.append((k, dy, inside(flow, flows) & inside(gy + dy, n_gy), (a, b, held(gy + dy, n_gy))))
         total = greet([(exists(dx, dy), neighbour(dx, dy)) for dx, dy in dirs]
-                      + [(always, ident) for _, ident in over_x + over_y]
-                      + [(ok, ident) for _, _, ok, ident in mates])
+                      + [(always, ident) for _, ident in over_x]
+                      + [(always, ring(d)) for d in (-1, 1)])
+        for _, _, ok, _ in mates:
+            total = total + ok.astype(jnp.int32)
 
         def clear(c0, c1, r0, r1):
             kb[:, c0:c1, r0:r1, :] = jnp.zeros((2, c1 - c0, r1 - r0, 128), jnp.float32)
@@ -474,12 +527,25 @@
         def _():
             clear(0, 14, 80, 88)
 
-        pl.semaphore_wait(barrier, total)
         for cp in loads:
             cp.wait()
+        pl.semaphore_wait(barrier, total)
+        for d in (-1, 1):
+            pl.semaphore_signal(tok.at[0, (d + 1) // 2], inc=1, device_id=ring(d), device_id_type=MESH)
         view = lambda c, r: kb.at[:, pl.ds(*c), pl.ds(*r), :]
         pending, recvs = halo(4, view, 4, 6, 4, neighbour, exists, True)
         run(pending)
+        for k, dy, ok, ident in mates:
+            @pl.when(ok)
+            def _(k=k, dy=dy, ident=ident):
+                pl.semaphore_signal(ready.at[1 - dy, (1, 1, 0, 0, 0, -1, -1)[k] + 1], inc=1, device_id=ident,
+                                    device_id_type=MESH)
+        for i, far in enumerate((2, 4, 0)):
+            for h in range(2):
+                pl.semaphore_wait(tok.at[i, h], 1)
+            if far:
+                for h in range(2):
+                    pl.semaphore_signal(tok.at[i + 1, h], inc=1, device_id=ring((2 * h - 1) * far), device_id_type=MESH)
         arrive(recvs)
 
         def weight(x, _):
@@ -662,7 +728,7 @@
         return pl.pallas_call(
             functools.partial(kernel, n_grp, n_gx, n_gy),
             out_shape=jax.ShapeDtypeStruct(drive.shape, jnp.float32),
-            in_specs=[pl.BlockSpec(memory_space=pl.ANY)] * 2,
+            in_specs=[pl.BlockSpec(memory_space=pltpu.HBM)] * 2,
             out_specs=pl.BlockSpec(memory_space=pltpu.VMEM),
             scratch_shapes=[
                 vmem(3, 6, ROWS, 128), vmem(4, 6, ROWS, 128), vmem(4, 6, ROWS, 128),
@@ -671,11 +737,12 @@
                 vmem(14, ROWS, 128), vmem(14, ROWS, 128), vmem(14, ROWS, 128), vmem(14, ROWS, 128),
                 vmem(128, 128), vmem(32, 128),
                 vmem(4, 8, 1, 128), vmem(24, 1, 128), vmem(4, 3, 3, 1, 128), vmem(24, 1, 128),
-                vmem(2, 8, 2, 8, 128), vmem(2, 32, 1, 128),
+                vmem(2, 8, 2, 8, 128), vmem(2, 32, 1, 128), vmem(4, 5, 9, 1, 128), vmem(32, 1, 128),
                 dma(4), dma(5, 9), dma(5, 9), dma(2, 8), dma(2, 8), dma(2, 16), dma(2, 16),
-                dma(3, 7), dma(3, 7), dma(21), dma(3, 3),
+                dma(3, 7), dma(3, 7), dma(21), dma(3, 3), dma(3, 5), dma(3, 5),
+                pltpu.SemaphoreType.REGULAR((3, 2)), pltpu.SemaphoreType.REGULAR((3, 3)),
             ],
-            compiler_params=pltpu.CompilerParams(collective_id=0, has_side_effects=True, vmem_limit_bytes=40 * 1024 * 1024),
+            compiler_params=pltpu.CompilerParams(collective_id=0, has_side_effects=True),
             name="coupling",
         )(drive, permeability)
 

time: 49.4 us -> 45.1 us (0.913)
  the two profiles are of different devices: /device:TPU:6 before, /device:TPU:1 now
where the time goes in v2:
time: 45.1 us; the launch traced here: 45 us
  Pallas kernels  43.3 us (96%)
  local copies, waits for them, and re-layouts  1.62 us (4%)
    pallas_call x1, Pallas kernels, per_device(): pl.pallas_call(functools.partial(kernel, n_grp, n_gx, n_gy), out_shape=ja...  43.3 us
    unnamed x1, local copies, waits for them, and re-layouts  1.62 us

profile of v2, /device:TPU:1, one launch (start us, length us, event | category | flops | bytes accessed | tf_op | source)
XLA Modules:
  0.0 45.0 jit_solution(8425127615451986149)
XLA Ops:
  0.0 43.3 %coupling.1 = f32[3,2,64,128]{3,2,1,0:T(8,128)} custom-call(f32[3,2,64,128]{3,2,1,0:T(8,128)} %drive.1, f32[6,64,128]{2,1,0:T(8,128)} %perm.1), custom_call_target="tpu_custom_call" | custom-call | tf_op jit(solution)/shard_map/coupling/pallas_call | solution.py:728
  43.3 1.6 %copy.4 = f32[3,2,64,128]{3,2,1,0:T(8,128)} copy(f32[3,2,64,128]{3,2,1,0:T(8,128)} %coupling.1) | data formatting | bytes 393216

commit v3 on v2

--- a/solution.py
+++ b/solution.py
@@ -109,7 +109,7 @@
 
 def kernel(n_grp, n_gx, n_gy, drive, perm, out, fb, e2, e3, e4, tmp, kb, w, v1, v2, v3, b2, mt, zt,
            surf, spb, infl, infs, ar1, ar2, nb, nbs,
-           lsem, hs, hr, a1s, a1r, a2s, a2r, sus, sur, ins, inr, ns, nr, tok, ready):
+           lsem, hs, hr, a1s, a1r, a2s, a2r, sus, sur, ins, inr, ns, nr, fs, fr, tok, ready):
     grp = lax.axis_index("grp")
     gx = lax.axis_index("gx")
     gy = lax.axis_index("gy")
@@ -201,7 +201,7 @@
     def _():
         infl[...] = jnp.zeros_like(infl)
         nb[...] = jnp.zeros_like(nb)
-        load = pltpu.make_async_copy(drive, fb.at[:, 2:4, 16:80, :], lsem.at[0])
+        load = pltpu.make_async_copy(drive, fb.at[:, 4:6, 16:80, :], lsem.at[0])
         load.start()
 
         def neighbour(dx, dy):
@@ -221,38 +221,50 @@
                     ok = ok & (r_of >= 1)
                 beds.append((dm, dy, ok, (n_grp - 1, held(m_of + dm, n_gx), held(gy + dy, n_gy))))
 
-        around = [(o, dy) for o in range(-2, 3) for dy in (-1, 0, 1) if (o, dy) != (0, 0)]
+        around = [(o, dy) for o in (-2, 2, -1, 1, 0) for dy in (-1, 1, 0) if (o, dy) != (0, 0)]
         total = greet([(exists(o, dy), neighbour(o, dy)) for o, dy in around])
         greet([(ok, ident) for _, _, ok, ident in beds])
 
-        def clear(c0, c1, r0, r1):
-            for buf in (fb, e2, e3, e4):
+        def clear(bufs, c0, c1, r0, r1):
+            for buf in bufs:
                 buf[:, c0:c1, r0:r1, :] = jnp.zeros((buf.shape[0], c1 - c0, r1 - r0, 128), jnp.float32)
 
+        @pl.when(j <= 1)
+        def _():
+            clear((fb,), 1, 2, 8, 88)
+
         @pl.when(j == 0)
         def _():
-            clear(0, 2, 8, 88)
+            clear((fb,), 2, 4, 8, 88)
+            clear((e3, e4), 0, 2, 8, 88)
+
+        @pl.when(j >= flows - 2)
+        def _():
+            clear((fb,), 8, 9, 8, 88)
 
         @pl.when(j == flows - 1)
         def _():
-            clear(4, 6, 8, 88)
+            clear((fb,), 6, 8, 8, 88)
+            clear((e3, e4), 4, 6, 8, 88)
 
         @pl.when(gy == 0)
         def _():
-            clear(0, 6, 8, 16)
+            clear((fb,), 1, 9, 8, 16)
+            clear((e3, e4), 0, 6, 8, 16)
 
         @pl.when(gy == n_gy - 1)
         def _():
-            clear(0, 6, 80, 88)
+            clear((fb,), 1, 9, 80, 88)
+            clear((e3, e4), 0, 6, 80, 88)
 
         load.wait()
 
         tiles = []
         for c in range(2):
             for t in OWN:
-                acc = fb[0, 2 + c, 8 * t:8 * t + 8, :]
+                acc = fb[0, 4 + c, 8 * t:8 * t + 8, :]
                 for f in (1, 2):
-                    acc = jnp.where(lane >= 3 * f, pltpu.roll(fb[f, 2 + c, 8 * t:8 * t + 8, :], 3 * f, 1), acc)
+                    acc = jnp.where(lane >= 3 * f, pltpu.roll(fb[f, 4 + c, 8 * t:8 * t + 8, :], 3 * f, 1), acc)
                 tiles.append(acc)
         turned = jnp.concatenate(tiles, axis=0).T
         for q in range(9):
@@ -266,19 +278,27 @@
                                                  nr.at[1 + dy, 2 + o], neighbour(o, dy))))
         run(low_out)
 
-        def begin(e, buf, wide, corners):
+        def exchange(e, buf, wide, corners):
             view = lambda c, r: buf.at[:, pl.ds(*c), pl.ds(*r), :]
             sends, recvs = halo(e, view, 2, 2, wide, neighbour, exists, corners)
             run(sends)
-            return sends, recvs
-
-        def exchange(e, buf, wide, corners):
-            sends, recvs = begin(e, buf, wide, corners)
             arrive(recvs)
             return sends
 
-        pending, recvs0 = begin(0, fb, 2, True)
-        pending = pending + low_out
+        sends0, recvs0 = [], []
+        for o, dy in around:
+            if abs(o) == 2 and dy != 0:
+                continue
+            sc, dc = {-2: ((4, 1), (8, 1)), -1: ((4, 2), (6, 2)), 0: ((4, 2), (4, 2)),
+                      1: ((4, 2), (2, 2)), 2: ((5, 1), (1, 1))}[o]
+            sr, dr = {-1: ((16, 8), (80, 8)), 0: ((16, 64), (16, 64)), 1: ((72, 8), (8, 8))}[dy]
+            src = fb.at[:, pl.ds(*sc), pl.ds(*sr), :]
+            dst = fb.at[:, pl.ds(*dc), pl.ds(*dr), :]
+            pair = fs.at[dy + 1, o + 2], fr.at[dy + 1, o + 2]
+            sends0.append((exists(o, dy), remote(src, dst, *pair, neighbour(o, dy))))
+            recvs0.append((exists(-o, -dy), remote(src, dst, *pair, neighbour(-o, -dy))))
+        run(sends0)
+        pending = sends0 + low_out
 
         even = lax.rem(sub, 2) == 0
         column = j * 2 - 3 + sub
@@ -389,8 +409,8 @@
                     r = 8 * t
                     div = None
                     for f in range(3):
-                        c = fb[f, x, pl.ds(r, 8), :]
-                        we, ea, so, no = near(fb, f, x, r)
+                        c = fb[f, x + 2, pl.ds(r, 8), :]
+                        we, ea, so, no = near(fb, f, x + 2, r)
                         be = below(c)
                         total = ((we + ea) + (so + no)) + (be + above(c))
                         dst[f, x, pl.ds(r, 8), :] = jnp.where(valid(x, t), (1.2 * C) * c + CC * total, 0.0)
@@ -412,7 +432,7 @@
                         we, ea, so, no = near(src, f, x, r)
                         be = below(c)
                         total = ((we + ea) + (so + no)) + (be + above(c))
-                        total = total + (fb[f, x, pl.ds(r, 8), :] - (toward[f] - p))
+                        total = total + (fb[f, x + 2, pl.ds(r, 8), :] - (toward[f] - p))
                         new = 0.2 * c + C * total
                         put(f, x, r, jnp.where(valid(x, t), new, 0.0) if masked else new)
                         part = c - (we, so, be)[f]
@@ -431,9 +451,8 @@
             if f < 3:
                 out[f, x - 2, pl.ds(r - 16, 8), :] = value
 
-        first_sweep(tmp, (1, 5), WIDE)
-        sweep(tmp, into(e2), (2, 4), OWN, False)
-        pending += exchange(1, e2, 1, False)
+        first_sweep(tmp, (0, 6), WIDE)
+        sweep(tmp, into(e2), (1, 5), WIDE, True)
         sweep(e2, into(e3), (2, 4), OWN, False)
 
         pending += exchange(2, e3, 2, True)
@@ -495,7 +514,7 @@
             return (n_grp - 1, gx, lax.rem(gy + d + n_gy, n_gy))
 
         over_x = [(d, (n_grp - 1, lax.rem(gx + d, n_gx), gy)) for d in range(1, n_gx)]
-        over_y = [(d, (n_grp - 1, gx, lax.rem(gy + d, n_gy))) for d in range(1, n_gy)]
+        over_y = [(d, (n_grp - 1, gx, lax.rem(gy + d, n_gy))) for d in sorted(range(1, n_gy), key=lambda d: -min(d, n_gy - d))]
         mates = []
         for k in range(7):
             flow = 3 * gx - 2 + k
@@ -540,12 +559,11 @@
             def _(k=k, dy=dy, ident=ident):
                 pl.semaphore_signal(ready.at[1 - dy, (1, 1, 0, 0, 0, -1, -1)[k] + 1], inc=1, device_id=ident,
                                     device_id_type=MESH)
-        for i, far in enumerate((2, 4, 0)):
+        for i, far in enumerate((2, 4)):
             for h in range(2):
                 pl.semaphore_wait(tok.at[i, h], 1)
-            if far:
-                for h in range(2):
-                    pl.semaphore_signal(tok.at[i + 1, h], inc=1, device_id=ring((2 * h - 1) * far), device_id_type=MESH)
+            for h in range(2):
+                pl.semaphore_signal(tok.at[i + 1, h], inc=1, device_id=ring((2 * h - 1) * far), device_id_type=MESH)
         arrive(recvs)
 
         def weight(x, _):
@@ -668,6 +686,8 @@
                 tiles.append(acc)
         zt[...] = jnp.concatenate(tiles, axis=0).T[0:32, :]
 
+        for h in range(2):
+            pl.semaphore_wait(tok.at[2, h], 1)
         first_y = spread_y(0, first_x)
 
         for k, dy, ok, ident in mates:
@@ -731,7 +751,7 @@
             in_specs=[pl.BlockSpec(memory_space=pltpu.HBM)] * 2,
             out_specs=pl.BlockSpec(memory_space=pltpu.VMEM),
             scratch_shapes=[
-                vmem(3, 6, ROWS, 128), vmem(4, 6, ROWS, 128), vmem(4, 6, ROWS, 128),
+                vmem(3, 10, ROWS, 128), vmem(4, 6, ROWS, 128), vmem(4, 6, ROWS, 128),
                 vmem(4, 6, ROWS, 128), vmem(4, 6, ROWS, 128),
                 vmem(2, 14, ROWS, 128), vmem(3, 14, ROWS, 128),
                 vmem(14, ROWS, 128), vmem(14, ROWS, 128), vmem(14, ROWS, 128), vmem(14, ROWS, 128),
@@ -739,12 +759,12 @@
                 vmem(4, 8, 1, 128), vmem(24, 1, 128), vmem(4, 3, 3, 1, 128), vmem(24, 1, 128),
                 vmem(2, 8, 2, 8, 128), vmem(2, 32, 1, 128), vmem(4, 5, 9, 1, 128), vmem(32, 1, 128),
                 dma(4), dma(5, 9), dma(5, 9), dma(2, 8), dma(2, 8), dma(2, 16), dma(2, 16),
-                dma(3, 7), dma(3, 7), dma(21), dma(3, 3), dma(3, 5), dma(3, 5),
+                dma(3, 7), dma(3, 7), dma(21), dma(3, 3), dma(3, 5), dma(3, 5), dma(3, 5), dma(3, 5),
                 pltpu.SemaphoreType.REGULAR((3, 2)), pltpu.SemaphoreType.REGULAR((3, 3)),
             ],
-            compiler_params=pltpu.CompilerParams(collective_id=0, has_side_effects=True),
+            compiler_params=pltpu.CompilerParams(collective_id=0, has_side_effects=True, vmem_limit_bytes=40 * 1024 * 1024),
             name="coupling",
-        )(drive, permeability)
+        )(pltpu.with_memory_space_constraint(drive, pltpu.HBM), pltpu.with_memory_space_constraint(permeability, pltpu.HBM))
 
     return jax.shard_map(
         per_device,

time: 45.1 us -> 41.9 us (0.929)
  Pallas kernels: 43.3 us -> 41.1 us
  local copies, waits for them, and re-layouts: 1.62 us -> 0.68 us
    pallas_call x1, Pallas kernels: 43.3 us -> 41.1 us  [per_device(): pl.pallas_call(functools.partial(kernel, n_grp, n_gx, n_gy), out_shape=ja...]
    unnamed x1, local copies, waits for them, and re-layouts: 1.62 us -> 0.68 us
where the time goes in v3:
time: 41.9 us; the launch traced here: 41.8 us
  Pallas kernels  41.1 us (98%)
  local copies, waits for them, and re-layouts  0.68 us (2%)
    pallas_call x1, Pallas kernels, per_device(): pl.pallas_call(functools.partial(kernel, n_grp, n_gx, n_gy), out_shape=ja...  41.1 us

profile of v3, /device:TPU:1, one launch (start us, length us, event | category | flops | bytes accessed | tf_op | source)
XLA Modules:
  0.0 41.8 jit_solution(17229659138970377027)
XLA Ops:
  0.0 41.1 %coupling.1 = f32[3,2,64,128]{3,2,1,0:T(8,128)S(1)} custom-call(f32[3,2,64,128]{3,2,1,0:T(8,128)} %drive.1, f32[6,64,128]{2,1,0:T(8,128)} %perm.1), custom_call_target="tpu_custom_call" | custom-call | tf_op jit(solution)/shard_map/coupling/pallas_call | solution.py:748
  41.1 0.7 %copy.4 = f32[3,2,64,128]{3,2,1,0:T(8,128)} copy(f32[3,2,64,128]{3,2,1,0:T(8,128)S(1)} %coupling.1) | data formatting | bytes 393216

commit v4 on v3

--- a/solution.py
+++ b/solution.py
@@ -109,7 +109,7 @@
 
 def kernel(n_grp, n_gx, n_gy, drive, perm, out, fb, e2, e3, e4, tmp, kb, w, v1, v2, v3, b2, mt, zt,
            surf, spb, infl, infs, ar1, ar2, nb, nbs,
-           lsem, hs, hr, a1s, a1r, a2s, a2r, sus, sur, ins, inr, ns, nr, fs, fr, tok, ready):
+           lsem, hs, hr, a1s, a1r, a2s, a2r, sus, sur, ins, inr, ns, nr, fs, fr, tok):
     grp = lax.axis_index("grp")
     gx = lax.axis_index("gx")
     gy = lax.axis_index("gy")
@@ -199,8 +199,6 @@
 
     @pl.when(jnp.logical_not(is_bed))
     def _():
-        infl[...] = jnp.zeros_like(infl)
-        nb[...] = jnp.zeros_like(nb)
         load = pltpu.make_async_copy(drive, fb.at[:, 4:6, 16:80, :], lsem.at[0])
         load.start()
 
@@ -221,9 +219,10 @@
                     ok = ok & (r_of >= 1)
                 beds.append((dm, dy, ok, (n_grp - 1, held(m_of + dm, n_gx), held(gy + dy, n_gy))))
 
-        around = [(o, dy) for o in (-2, 2, -1, 1, 0) for dy in (-1, 1, 0) if (o, dy) != (0, 0)]
+        around = [(o, dy) for o in (-2, 2, -1, 1, 0) for dy in (-1, 1, 0) if (o, dy) != (0, 0) and (abs(o) < 2 or dy == 0)]
         total = greet([(exists(o, dy), neighbour(o, dy)) for o, dy in around])
-        greet([(ok, ident) for _, _, ok, ident in beds])
+        for _, _, ok, _ in beds:
+            total = total + ok.astype(jnp.int32)
 
         def clear(bufs, c0, c1, r0, r1):
             for buf in bufs:
@@ -287,8 +286,6 @@
 
         sends0, recvs0 = [], []
         for o, dy in around:
-            if abs(o) == 2 and dy != 0:
-                continue
             sc, dc = {-2: ((4, 1), (8, 1)), -1: ((4, 2), (6, 2)), 0: ((4, 2), (4, 2)),
                       1: ((4, 2), (2, 2)), 2: ((5, 1), (1, 1))}[o]
             sr, dr = {-1: ((16, 8), (80, 8)), 0: ((16, 64), (16, 64)), 1: ((72, 8), (8, 8))}[dy]
@@ -369,6 +366,8 @@
                 q = 3 * f + z
 
                 def row(i, o, q=q):
+                    if abs(o) == 2 and i != 1:
+                        return jnp.zeros((8, 128), jnp.float32)
                     one = nbs[8 + q] if (i, o) == (1, 0) else nb[i, o + 2, q]
                     return jnp.broadcast_to(one, (8, 128))
                 force[f][z] = assemble(row)
@@ -379,9 +378,6 @@
         spb[8] = jnp.where(lane[0:1] < 64, pltpu.roll(low, 96, 1)[3:4], pltpu.roll(low, 32, 1)[4:5])
         tells = []
         for dm, dy, ok, ident in beds:
-            @pl.when(ok)
-            def _(dm=dm, dy=dy):
-                pl.semaphore_wait(ready.at[1 + dy, dm + 1], 1)
             for r in range(3):
                 slot = r + 2 - 3 * dm
                 if 0 <= slot < 7:
@@ -463,11 +459,13 @@
         sweep(tmp, final, (2, 4), OWN, False)
 
         for dm, dy, ok, ident in beds:
-            @pl.when(ok)
+            @pl.when(ok if dm == 0 or dy == 0 else ok & (r_of != 1))
             def _(dm=dm, dy=dy, ident=ident):
                 remote(infs.at[8:11], infl.at[1 + dy, dm + 1], ins.at[0], inr.at[1 + dy, dm + 1], ident).wait_recv()
 
         def row(i, o):
+            if abs(o) == 2 and i != 1:
+                return jnp.zeros((8, 128), jnp.float32)
             pick = [jnp.broadcast_to(infl[i, (r + o + 3) // 3, (r + o + 3) % 3], (8, 128)) for r in range(3)]
             return jnp.where(r_of == 0, pick[0], jnp.where(r_of == 1, pick[1], pick[2]))
 
@@ -524,8 +522,7 @@
         total = greet([(exists(dx, dy), neighbour(dx, dy)) for dx, dy in dirs]
                       + [(always, ident) for _, ident in over_x]
                       + [(always, ring(d)) for d in (-1, 1)])
-        for _, _, ok, _ in mates:
-            total = total + ok.astype(jnp.int32)
+        greet([(ok, ident) for _, _, ok, ident in mates])
 
         def clear(c0, c1, r0, r1):
             kb[:, c0:c1, r0:r1, :] = jnp.zeros((2, c1 - c0, r1 - r0, 128), jnp.float32)
@@ -554,11 +551,6 @@
         view = lambda c, r: kb.at[:, pl.ds(*c), pl.ds(*r), :]
         pending, recvs = halo(4, view, 4, 6, 4, neighbour, exists, True)
         run(pending)
-        for k, dy, ok, ident in mates:
-            @pl.when(ok)
-            def _(k=k, dy=dy, ident=ident):
-                pl.semaphore_signal(ready.at[1 - dy, (1, 1, 0, 0, 0, -1, -1)[k] + 1], inc=1, device_id=ident,
-                                    device_id_type=MESH)
         for i, far in enumerate((2, 4)):
             for h in range(2):
                 pl.semaphore_wait(tok.at[i, h], 1)
@@ -727,6 +719,8 @@
         tells = []
         for k, dy, ok, ident in mates:
             dm = (1, 1, 0, 0, 0, -1, -1)[k]
+            if k in (0, 6) and dy != 0:
+                continue
             tells.append((ok, remote(infs.at[8:11], infl.at[1 - dy, dm + 1], ins.at[k * 3 + dy + 1], inr.at[1 - dy, dm + 1], ident)))
         run(tells)
         c2 = solve(1, second_y)
@@ -760,7 +754,7 @@
                 vmem(2, 8, 2, 8, 128), vmem(2, 32, 1, 128), vmem(4, 5, 9, 1, 128), vmem(32, 1, 128),
                 dma(4), dma(5, 9), dma(5, 9), dma(2, 8), dma(2, 8), dma(2, 16), dma(2, 16),
                 dma(3, 7), dma(3, 7), dma(21), dma(3, 3), dma(3, 5), dma(3, 5), dma(3, 5), dma(3, 5),
-                pltpu.SemaphoreType.REGULAR((3, 2)), pltpu.SemaphoreType.REGULAR((3, 3)),
+                pltpu.SemaphoreType.REGULAR((3, 2)),
             ],
             compiler_params=pltpu.CompilerParams(collective_id=0, has_side_effects=True, vmem_limit_bytes=40 * 1024 * 1024),
             name="coupling",

time: 41.9 us -> 40.9 us (0.976)
  Pallas kernels: 41.1 us -> 40.1 us
    pallas_call x1, Pallas kernels: 41.1 us -> 40.1 us  [per_device(): pl.pallas_call(functools.partial(kernel, n_grp, n_gx, n_gy), out_shape=ja...]
where the time goes in v4:
time: 40.9 us; the launch traced here: 40.8 us
  Pallas kernels  40.1 us (98%)
  local copies, waits for them, and re-layouts  0.68 us (2%)
    pallas_call x1, Pallas kernels, per_device(): pl.pallas_call(functools.partial(kernel, n_grp, n_gx, n_gy), out_shape=ja...  40.1 us

profile of v4, /device:TPU:1, one launch (start us, length us, event | category | flops | bytes accessed | tf_op | source)
XLA Modules:
  0.0 40.8 jit_solution(9242762650703063180)
XLA Ops:
  0.0 40.1 %coupling.1 = f32[3,2,64,128]{3,2,1,0:T(8,128)S(1)} custom-call(f32[3,2,64,128]{3,2,1,0:T(8,128)} %drive.1, f32[6,64,128]{2,1,0:T(8,128)} %perm.1), custom_call_target="tpu_custom_call" | custom-call | tf_op jit(solution)/shard_map/coupling/pallas_call | solution.py:742
  40.1 0.7 %copy.4 = f32[3,2,64,128]{3,2,1,0:T(8,128)} copy(f32[3,2,64,128]{3,2,1,0:T(8,128)S(1)} %coupling.1) | data formatting | bytes 393216

commit v5 on v4

--- a/solution.py
+++ b/solution.py
@@ -458,6 +458,7 @@
         sweep(e4, into(tmp), (1, 5), WIDE, True)
         sweep(tmp, final, (2, 4), OWN, False)
 
+        drain(pending)
         for dm, dy, ok, ident in beds:
             @pl.when(ok if dm == 0 or dy == 0 else ok & (r_of != 1))
             def _(dm=dm, dy=dy, ident=ident):
@@ -489,7 +490,6 @@
                 for c in range(2):
                     add = pltpu.roll(turn, (128 - 8 * (2 * f + c)) % 128, 1)
                     out[f, c, 8 * t:8 * t + 8, :] += jnp.where(lane < 8, add, 0.0)
-        drain(pending)
 
     @pl.when(is_bed)
     def _():
@@ -551,20 +551,13 @@
         view = lambda c, r: kb.at[:, pl.ds(*c), pl.ds(*r), :]
         pending, recvs = halo(4, view, 4, 6, 4, neighbour, exists, True)
         run(pending)
-        for i, far in enumerate((2, 4)):
-            for h in range(2):
-                pl.semaphore_wait(tok.at[i, h], 1)
-            for h in range(2):
-                pl.semaphore_signal(tok.at[i + 1, h], inc=1, device_id=ring((2 * h - 1) * far), device_id_type=MESH)
-        arrive(recvs)
-
-        def weight(x, _):
+        def weight(x, tiles):
             open_x = gx >= 0
             if x == 3:
                 open_x = gx > 0
             if x == 9:
                 open_x = gx < n_gx - 1
-            for t in WIDE:
+            for t in tiles:
                 r = 8 * t
                 k = kb[0, x, pl.ds(r, 8), :]
                 w[0, x, pl.ds(r, 8), :] = jnp.where(open_x, (k + kb[0, x + 1, pl.ds(r, 8), :]) * (0.5 * SCALE), 0.0)
@@ -576,9 +569,6 @@
                 w[1, x, pl.ds(r, 8), :] = wy
                 up = pltpu.roll(k, 127, 1)
                 w[2, x, pl.ds(r, 8), :] = jnp.where(l127, k * SCALE, (k + up) * (0.5 * SCALE))
-            return 0
-
-        loop(0, 13, weight, 0)
 
         def image(src, x, t):
             r = 8 * t
@@ -590,15 +580,36 @@
             gz = w[2, x, pl.ds(r, 8), :] * (f - above(f))
             return ((ge + gw) + (gn + gs)) + (gz - below(gz))
 
+        def source(x, r):
+            return kb[1, x, pl.ds(r, 8), :]
+
+        early = [(x, t) for x in range(5, 9) for t in range(3, 9)]
+        for x in range(4, 9):
+            weight(x, range(2, 9))
+        for x, t in early:
+            v1[x, pl.ds(8 * t, 8), :] = image(source, x, t)
+
+        for i, far in enumerate((2, 4)):
+            for h in range(2):
+                pl.semaphore_wait(tok.at[i, h], 1)
+            for h in range(2):
+                pl.semaphore_signal(tok.at[i + 1, h], inc=1, device_id=ring((2 * h - 1) * far), device_id_type=MESH)
+        arrive(recvs)
+
+        for x in range(13):
+            weight(x, [t for t in WIDE if not (4 <= x < 9 and 2 <= t < 9)])
+
         def reader(ref):
             return lambda x, r: ref[x, pl.ds(r, 8), :]
 
         r1, r2, r3 = reader(v1), reader(v2), reader(v3)
 
-        def powers(src):
+        def powers(src, done=()):
             for here, there, lo, hi in ((src, v1, 1, 13), (r1, v2, 2, 12), (r2, v3, 3, 11)):
                 def body(x, _, here=here, there=there):
                     for t in WIDE:
+                        if there is v1 and (x, t) in done:
+                            continue
                         there[x, pl.ds(8 * t, 8), :] = image(here, x, t)
                     return 0
                 loop(lo, hi, body, 0)
@@ -660,10 +671,7 @@
             mu = [quick(jnp.broadcast_to(th[i:i + 1], (8, 128)), jnp.broadcast_to(tl[i:i + 1], (8, 128))) for i in range(8)]
             return coefficients(mu)
 
-        def source(x, r):
-            return kb[1, x, pl.ds(r, 8), :]
-
-        first_x = spread_x(0, powers(source))
+        first_x = spread_x(0, powers(source, early))
 
         tiles = []
         for c in range(2):
@@ -723,6 +731,7 @@
                 continue
             tells.append((ok, remote(infs.at[8:11], infl.at[1 - dy, dm + 1], ins.at[k * 3 + dy + 1], inr.at[1 - dy, dm + 1], ident)))
         run(tells)
+        drain(pending + first_x + first_y + second_x + second_y + tells)
         c2 = solve(1, second_y)
 
         for x in range(4, 10):
@@ -730,7 +739,6 @@
                 rows8 = pl.ds(8 * t, 8)
                 total = (c2[0] * b2[x, rows8, :] + c2[1] * v1[x, rows8, :]) + (c2[2] * v2[x, rows8, :] + c2[3] * v3[x, rows8, :])
                 out[(x - 4) // 2, x % 2, pl.ds(8 * t - 16, 8), :] = total
-        drain(pending + first_x + first_y + second_x + second_y + tells)
 
 
 def solution(mesh):

time: 40.9 us -> 40.7 us (level)
  no operation moved by 1% of the time
where the time goes in v5:
time: 40.7 us; the launch traced here: 40.6 us
  Pallas kernels  39.9 us (98%)
  local copies, waits for them, and re-layouts  0.68 us (2%)
    pallas_call x1, Pallas kernels, per_device(): pl.pallas_call(functools.partial(kernel, n_grp, n_gx, n_gy), out_shape=ja...  39.9 us

profile of v5, /device:TPU:1, one launch (start us, length us, event | category | flops | bytes accessed | tf_op | source)
XLA Modules:
  0.0 40.6 jit_solution(15951168208855934336)
XLA Ops:
  0.0 39.9 %coupling.1 = f32[3,2,64,128]{3,2,1,0:T(8,128)S(1)} custom-call(f32[3,2,64,128]{3,2,1,0:T(8,128)} %drive.1, f32[6,64,128]{2,1,0:T(8,128)} %perm.1), custom_call_target="tpu_custom_call" | custom-call | tf_op jit(solution)/shard_map/coupling/pallas_call | solution.py:750
  39.9 0.7 %copy.4 = f32[3,2,64,128]{3,2,1,0:T(8,128)} copy(f32[3,2,64,128]{3,2,1,0:T(8,128)S(1)} %coupling.1) | data formatting | bytes 393216
